TPU v7x, 32 devices: a whole 2x2x4 slice. The times are simulated.
32 devices in a mesh: section: 4 (over z), gx: 2 (over x), gy: 2 (over y), gz: 2 (over core).
Axes of the slice: x: 2, y: 2, z: 4, core: 2. Of those that a mesh axis runs over, the one named last changes fastest.
Arguments:
- micro_inputs: bfloat16 [1, 256, 8192], P(None, 'gy', ('gx', 'gz')), may hold values from -40 to 40
- norm_gain: float32 [4, 8192], P('section', 'gx'), may hold values from 0.5 to 1.5
- q_weight: bfloat16 [4, 8192, 8192], P('section', ('gx', 'gy'), 'gz'), may hold values from -0.0625 to 0.0625
- kv_weight: bfloat16 [4, 2, 8192, 1024], P('section', None, ('gx', 'gy'), 'gz'), may hold values from -0.0625 to 0.0625
- q_bias: float32 [4, 8192], P('section', 'gz'), may hold values from -130 to 130
- kv_bias: float32 [4, 2, 1024], P('section', None, 'gz'), may hold values from -50 to 50
- out_weight: bfloat16 [4, 8192, 8192], P('section', 'gz', ('gx', 'gy')), may hold values from -0.0625 to 0.0625
Outputs:
- hidden_out: bfloat16 [4, 1, 256, 8192], P('section', None, 'gy', ('gx', 'gz'))
All inputs are finite; a program needn't handle non-finite values.
Results may differ from a plain program's by a relative error of at most 0.025.
Values may be sent and summed in bfloat16 or wider, within the bound.
No kernel may reach another device: no remote copies, remote signals or barrier semaphores. Data moves between devices by JAX's collectives and lax.ppermute only.
A program may use at most 128 MiB of HBM per device.

v0:
```python
import jax
import jax.numpy as jnp
from jax import lax
from jax.experimental import pallas as pl
from jax.experimental.pallas import tpu as pltpu
from jax.sharding import PartitionSpec as P

HD = 128
ROPE_BASE = 1000000.0
EPSILON = 1e-06
NEG_FILL = -1e30
CHUNKS = 2
HELD_BLOCKS = 3
WHOLE = pl.BlockSpec(memory_space=pltpu.VMEM)
SCALARS = pl.BlockSpec(memory_space=pltpu.SMEM)
LIMIT = pltpu.CompilerParams(vmem_limit_bytes=4 << 20)


def tile_of(columns):
    return 256 if columns % 256 == 0 else 128


def effort(flops, moved=0):
    return pl.CostEstimate(flops=flops, transcendentals=0, bytes_accessed=moved)


def resident(small, early, sources, copies, shapes):
    def kernel(*refs):
        small_refs = refs[: len(small)]
        source_refs = refs[len(small) : len(small) + len(sources)]
        outs = refs[len(small) + len(sources) + len(early) :]
        moves = []
        for i, (source, where, held, target) in enumerate(copies):
            where = where(small_refs[0]) if callable(where) else where
            moves.append(
                pltpu.make_async_copy(source_refs[source].at[where], outs[len(small) + held].at[target], outs[-1].at[i])
            )
        for move in moves:
            move.start()
        for value, ref, out in zip(small, small_refs, outs):
            if value.dtype == jnp.int32:
                for i in range(value.shape[0]):
                    out[i] = ref[i]
            else:
                out[...] = ref[...]
        for move in moves:
            move.wait()

    def space(value):
        return SCALARS if value.dtype == jnp.int32 else WHOLE

    return pl.pallas_call(
        kernel,
        out_shape=[(pltpu.SMEM if v.dtype == jnp.int32 else pltpu.VMEM)(v.shape, v.dtype) for v in small]
        + [pltpu.VMEM(shape, jnp.bfloat16) for shape in shapes],
        in_specs=[space(v) for v in small] + [pl.BlockSpec(memory_space=pltpu.HBM)] * len(sources)
        + [pl.BlockSpec(memory_space=pl.ANY)] * len(early),
        out_specs=[space(v) for v in small] + [WHOLE] * len(shapes),
        scratch_shapes=[pltpu.SemaphoreType.DMA((len(copies),))],
        compiler_params=pltpu.CompilerParams(vmem_limit_bytes=1 << 20),
        cost_estimate=effort(1 << 32),
    )(*small, *[pltpu.with_memory_space_constraint(x, pltpu.HBM) for x in sources], *early)


def project_into(o_ref, x_ref, w_ref, start, width):
    tile = tile_of(width)

    def step(i, _):
        o_ref[:, pl.ds(pl.multiple_of(i * tile, 128), tile)] = jnp.dot(
            x_ref[...],
            w_ref[:, pl.ds(pl.multiple_of(start + i * tile, 128), tile)],
            preferred_element_type=jnp.float32,
        ).astype(o_ref.dtype)
        return 0

    lax.fori_loop(0, width // tile, step, 0)


def project_block(table, slot, rows, weight, width, kind):
    def kernel(table_ref, x_ref, w_ref, o_ref):
        project_into(o_ref, x_ref, w_ref, table_ref[slot] * width, width)

    return pl.pallas_call(
        kernel,
        out_shape=jax.ShapeDtypeStruct((rows.shape[0], width), kind),
        in_specs=[SCALARS, WHOLE, WHOLE],
        out_specs=WHOLE,
        compiler_params=LIMIT,
        cost_estimate=effort(2 * rows.shape[0] * rows.shape[1] * width),
    )(table, rows, weight)


def enter(table, slot, pieces, gain, weight, width):
    count = len(pieces)
    share, slab = pieces[0].shape
    chunk = share * count

    def kernel(table_ref, gain_ref, w_ref, *refs):
        scaled_ref, total_ref, o_ref = refs[count:]
        totals = []
        for i in range(count):
            wide = refs[i][...].astype(jnp.float32)
            scaled_ref[i * share : (i + 1) * share, :] = (wide * gain_ref[...]).astype(jnp.bfloat16)
            totals.append(jnp.sum(wide * wide, axis=1, keepdims=True))
        total = jnp.broadcast_to(jnp.concatenate(totals, axis=0), (chunk, 128))
        total_ref[...] = jnp.transpose(total)[:8]
        project_into(o_ref, scaled_ref, w_ref, table_ref[slot] * width, width)

    return pl.pallas_call(
        kernel,
        out_shape=(
            jax.ShapeDtypeStruct((chunk, slab), jnp.bfloat16),
            jax.ShapeDtypeStruct((8, chunk), jnp.float32),
            jax.ShapeDtypeStruct((chunk, width), jnp.bfloat16),
        ),
        in_specs=[SCALARS] + [WHOLE] * (2 + count),
        out_specs=(WHOLE, WHOLE, WHOLE),
        compiler_params=LIMIT,
        cost_estimate=effort(2 * chunk * slab * width),
    )(table, gain, weight, *pieces)


def attend(projected, received, totals, bias, cosine, sine, mask, earlier, heads, used, features):
    chunk = projected.shape[0]
    group = heads // used
    own_cols = heads * HD
    used_cols = used * HD
    parts = len(received)
    past = len(earlier)
    scale = HD ** (-0.5)

    def kernel(p_ref, bias_ref, cos_ref, sin_ref, mask_ref, *refs):
        part_refs = refs[:parts]
        total_refs = refs[parts : 2 * parts + 1]
        past_refs = refs[2 * parts + 1 : 2 * parts + 1 + 2 * past]
        o_ref, k_ref, v_ref = refs[2 * parts + 1 + 2 * past :]
        total = total_refs[0][0:1, :]
        for ref in total_refs[1:]:
            total = total + ref[0:1, :]
        inverse = lax.rsqrt(total / features + EPSILON)
        inverse = jnp.transpose(jnp.broadcast_to(inverse, (HD, chunk)))
        cosine_rows = cos_ref[...]
        sine_rows = sin_ref[...]

        def columns(start):
            value = p_ref[:, start : start + HD]
            for ref in part_refs:
                value = value + ref[:, start : start + HD].astype(jnp.float32)
            return value * inverse + bias_ref[:, start : start + HD]

        def rotate(value):
            return (value * cosine_rows + pltpu.roll(value, HD // 2, 1) * sine_rows).astype(jnp.bfloat16)

        allowed = mask_ref[...] > 0.5
        for u in range(used):
            spot = slice(u * HD, (u + 1) * HD)
            k_ref[:, spot] = rotate(columns(own_cols + u * HD))
            v_ref[:, spot] = columns(own_cols + used_cols + u * HD).astype(jnp.bfloat16)
            keys = [k_ref[:, spot]] + [past_refs[2 * j][:, spot] for j in range(past)]
            values = [v_ref[:, spot]] + [past_refs[2 * j + 1][:, spot] for j in range(past)]
            keys = jnp.concatenate(keys, axis=0) if past else keys[0]
            values = jnp.concatenate(values, axis=0) if past else values[0]
            for g in range(group):
                start = (u * group + g) * HD
                query = rotate(columns(start))
                scores = (
                    lax.dot_general(query, keys, (((1,), (1,)), ((), ())), preferred_element_type=jnp.float32) * scale
                )
                scores = jnp.where(allowed, scores, NEG_FILL)
                weights = jnp.where(allowed, jnp.exp(scores - jnp.max(scores, axis=1, keepdims=True)), 0.0)
                denominator = jnp.sum(weights, axis=1, keepdims=True)
                mixed = jnp.dot(weights.astype(jnp.bfloat16), values, preferred_element_type=jnp.float32)
                o_ref[:, start : start + HD] = (mixed / denominator).astype(jnp.bfloat16)

    return pl.pallas_call(
        kernel,
        out_shape=(
            jax.ShapeDtypeStruct((chunk, own_cols), jnp.bfloat16),
            jax.ShapeDtypeStruct((chunk, used_cols), jnp.bfloat16),
            jax.ShapeDtypeStruct((chunk, used_cols), jnp.bfloat16),
        ),
        in_specs=[WHOLE] * (5 + 2 * parts + 1 + 2 * past),
        out_specs=(WHOLE, WHOLE, WHOLE),
        compiler_params=LIMIT,
        cost_estimate=effort(1 << 29),
    )(projected, bias, cosine, sine, mask, *received, *totals, *[a for pair in earlier for a in pair])


def mix_blocks(table, slots, blocks, weight, held, so_far, cores):
    count = len(blocks)
    chunk, depth = blocks[0].shape
    slab = weight.shape[2]
    share = chunk // cores
    tile = min(slab, 512)
    near = [b for b in range(count) if slots[b] in held]
    steps = [(i, b) for i in range(slab // tile) for b in range(count) if b not in near]
    buffers = min(4, len(steps))
    ready = [held[slots[b]] for b in near]
    inputs = [*blocks, *ready] + ([] if so_far is None else [so_far])

    def kernel(table_ref, w_ref, *refs):
        outs = refs[len(inputs) : len(inputs) + cores]
        fetches = []
        for step, (i, b) in enumerate(steps):
            row = pl.multiple_of(table_ref[slots[b]] * depth, 128)
            buffer, sems = refs[-2:]
            fetches.append(
                pltpu.make_async_copy(
                    w_ref.at[0, pl.ds(row, depth), pl.ds(i * tile, tile)],
                    buffer.at[step % buffers],
                    sems.at[step % buffers],
                )
            )
        for fetch in fetches[:buffers]:
            fetch.start()
        for i in range(slab // tile):
            spot = slice(i * tile, (i + 1) * tile)
            out = None if so_far is None else refs[len(inputs) - 1][:, spot]
            for b in near + [b for b in range(count) if b not in near]:
                if b in near:
                    rows = refs[count + near.index(b)][:, spot]
                else:
                    step = steps.index((i, b))
                    fetches[step].wait()
                    rows = refs[-2][step % buffers]
                term = jnp.dot(refs[b][...], rows, preferred_element_type=jnp.float32)
                out = term if out is None else out + term
                if b not in near and step + buffers < len(steps):
                    fetches[step + buffers].start()
            for j, ref in enumerate(outs):
                ref[:, spot] = out[j * share : (j + 1) * share].astype(ref.dtype)

    scratch = [pltpu.VMEM((buffers, depth, tile), jnp.bfloat16), pltpu.SemaphoreType.DMA((buffers,))]
    return pl.pallas_call(
        kernel,
        out_shape=[
            jax.ShapeDtypeStruct((share, slab), jnp.bfloat16 if j else jnp.float32) for j in range(cores)
        ],
        in_specs=[SCALARS, pl.BlockSpec(memory_space=pltpu.HBM)] + [WHOLE] * len(inputs),
        out_specs=[WHOLE] * cores,
        scratch_shapes=scratch if steps else [],
        compiler_params=pltpu.CompilerParams(vmem_limit_bytes=8 << 20),
        cost_estimate=effort(2 * count * chunk * depth * slab),
    )(table, weight, *inputs)


def leave(rows, own_sum, pieces):
    def kernel(x_ref, sum_ref, *refs):
        value = x_ref[...].astype(jnp.float32) + sum_ref[...]
        for ref in refs[:-1]:
            value = value + ref[...].astype(jnp.float32)
        refs[-1][...] = value.astype(jnp.bfloat16)

    return pl.pallas_call(
        kernel,
        out_shape=jax.ShapeDtypeStruct(rows.shape, jnp.bfloat16),
        in_specs=[WHOLE] * (2 + len(pieces)),
        out_specs=WHOLE,
        compiler_params=LIMIT,
        cost_estimate=effort(1 << 26),
    )(rows, own_sum, *pieces)


def around(value, axis, steps):
    count = lax.axis_size(axis)
    return lax.ppermute(value, axis, [(i, (i + steps) % count) for i in range(count)])


def gathered(value, axis, dim):
    pieces = [value] + [around(value, axis, -j) for j in range(1, lax.axis_size(axis))]
    count = lax.axis_size(axis)
    stacked = jnp.take(jnp.stack(pieces), (jnp.arange(count) - lax.axis_index(axis)) % count, axis=0)
    shape = list(value.shape)
    shape[dim] *= count
    return jnp.moveaxis(stacked, 0, dim).reshape(shape)


def body(micro_inputs, norm_gain, q_weight, kv_weight, q_bias, kv_bias, out_weight):
    sections = lax.axis_size("section")
    size_gx, size_gy, size_gz = (lax.axis_size(a) for a in ("gx", "gy", "gz"))
    group = size_gx * size_gy
    index_gx, index_gy, index_gz = (lax.axis_index(a) for a in ("gx", "gy", "gz"))
    index_section = lax.axis_index("section")
    me = index_gx * size_gy + index_gy
    micro_count = micro_inputs.shape[0]
    tokens = micro_inputs.shape[1] * size_gy
    features = micro_inputs.shape[2] * size_gx * size_gz
    slab = q_weight.shape[1]
    chunk = tokens // CHUNKS
    share = chunk // size_gz
    q_cols = q_weight.shape[2]
    kv_cols = kv_weight.shape[3]
    group_size = q_cols // kv_cols
    own_cols = q_cols // group
    own_heads = own_cols // HD
    used_heads = max(1, own_heads // group_size)
    used_cols = used_heads * HD
    width = own_cols + 2 * used_cols
    jobs = micro_count * CHUNKS

    offsets = [(dx, dy) for dx in range(size_gx) for dy in range(size_gy)][1:]
    offsets.sort(key=lambda o: (min(o[0], size_gx - o[0]) + min(o[1], size_gy - o[1])))

    def chip_at(dx, dy):
        x = index_gx + dx
        y = index_gy + dy
        return jnp.where(x >= size_gx, x - size_gx, x) * size_gy + jnp.where(y >= size_gy, y - size_gy, y)

    def to_offset(value, dx, dy):
        pairs = [
            (x * size_gy + y, (x + dx) % size_gx * size_gy + (y + dy) % size_gy)
            for x in range(size_gx)
            for y in range(size_gy)
        ]
        return lax.ppermute(value, ("gx", "gy"), pairs)

    def kv_start(chip):
        return chip * own_heads // group_size * HD

    even = size_gy == size_gz == CHUNKS
    if even:

        def spread(block):
            cut = block.reshape(size_gz, share, slab)
            pieces = []
            for j in range(CHUNKS):
                spot = lax.rem(index_gy + j, size_gz)
                pairs = [
                    (a * size_gz + b, b * size_gz + (a + j) % size_gz) for a in range(size_gy) for b in range(size_gz)
                ]
                piece = lax.dynamic_index_in_dim(cut, spot, 0, keepdims=False)
                pieces.append(lax.ppermute(piece, ("gy", "gz"), pairs))
            return [
                sum_of([(lax.rem(index_gz + size_gz - j, size_gz) == k, pieces[j]) for j in range(CHUNKS)])
                for k in range(CHUNKS)
            ]

        def collect(slabs):
            pieces = []
            for j in range(CHUNKS):
                pairs = [
                    (c * size_gz + d, (d + j) % size_gy * size_gz + c) for c in range(size_gy) for d in range(size_gz)
                ]
                piece = sum_of([(flag(sections + j * CHUNKS + k), slabs[k]) for k in range(CHUNKS)])
                pieces.append(lax.ppermute(piece, ("gy", "gz"), pairs))
            return jnp.concatenate(
                [
                    sum_of([(flag(sections + CHUNKS * CHUNKS + d * CHUNKS + j), pieces[j]) for j in range(CHUNKS)])
                    for d in range(size_gz)
                ],
                axis=0,
            )
    else:

        def spread(block):
            wide = gathered(block, "gz", 1)
            pieces = lax.all_to_all(wide, "gy", split_axis=1, concat_axis=0, tiled=True)
            pieces = pieces.reshape(CHUNKS, size_gz, share, slab)
            pieces = lax.dynamic_index_in_dim(pieces, index_gz, 1, keepdims=False)
            return [pieces[k] for k in range(CHUNKS)]

        def collect(slabs):
            rows = gathered(jnp.stack(slabs), "gz", 1).reshape(tokens, slab)
            wide = lax.all_to_all(rows, "gy", split_axis=0, concat_axis=1, tiled=True)
            piece = wide.shape[1] // size_gz
            return lax.dynamic_slice_in_dim(wide, index_gz * piece, piece, 1)

    def sum_of(choices):
        chosen = choices[0][1]
        for condition, value in choices[1:]:
            chosen = jnp.where(condition, value, chosen)
        return chosen

    entering = [piece for m in range(micro_count) for piece in spread(micro_inputs[m])]

    gain_slab = lax.dynamic_slice_in_dim(norm_gain[0], index_gy * slab, slab, 0)[None, :]
    own_bias = jnp.concatenate(
        [
            lax.dynamic_slice_in_dim(q_bias[0], me * own_cols, own_cols, 0),
            lax.dynamic_slice_in_dim(kv_bias[0, 0], kv_start(me), used_cols, 0),
            lax.dynamic_slice_in_dim(kv_bias[0, 1], kv_start(me), used_cols, 0),
        ]
    )[None, :]

    order = (index_gz + jnp.arange(size_gz)) % size_gz
    row_pos = (order[:, None] * share + jnp.arange(share)[None, :]).reshape(chunk)
    half_width = HD // 2
    frequency = ROPE_BASE ** (-jnp.arange(half_width, dtype=jnp.float32) * 2.0 / HD)
    ticks = jobs + sections - 1
    ordinals = (jnp.arange(ticks) - index_section) % CHUNKS
    positions = ordinals[:, None] * chunk + row_pos[None, :]
    angles = positions.astype(jnp.float32)[:, :, None] * frequency[None, None, :]
    cosines = jnp.cos(angles)
    sines = jnp.sin(angles)
    cosines = list(jnp.concatenate([cosines, cosines], axis=-1))
    sines = list(jnp.concatenate([-sines, sines], axis=-1))
    causal = row_pos[None, :] <= row_pos[:, None]
    masks = [
        jnp.concatenate(
            [causal] + [jnp.broadcast_to(ordinals[t] >= j, (chunk, chunk)) for j in range(1, min(CHUNKS, t + 1))],
            axis=1,
        ).astype(jnp.float32)
        for t in range(ticks)
    ]
    conditions = [index_section == s for s in range(sections)]
    if even:
        conditions += [lax.rem(index_gz + j, size_gy) == k for j in range(CHUNKS) for k in range(CHUNKS)]
        conditions += [lax.rem(index_gy + size_gy - j, size_gz) == d for d in range(size_gz) for j in range(CHUNKS)]
    flags = jnp.broadcast_to(jnp.stack(conditions).astype(jnp.float32)[:, None], (len(conditions), 128))
    far_first = offsets[::-1]
    targets = [chip_at(dx, dy) for dx, dy in far_first]
    sources = [chip_at(size_gx - dx if dx else 0, size_gy - dy if dy else 0) for dx, dy in offsets]
    table = jnp.stack(targets + sources + [me]).astype(jnp.int32)
    mine = 2 * len(offsets)
    copies = []
    everything = slice(None)
    for chip in range(group):
        kv_from = chip * own_heads // group_size * HD
        target = (everything, pl.ds(chip * width, own_cols))
        copies.append((0, (0, everything, pl.ds(chip * own_cols, own_cols)), 0, target))
        for i in range(2):
            target = (everything, pl.ds(chip * width + own_cols + i * used_cols, used_cols))
            copies.append((1, (0, i, everything, pl.ds(kv_from, used_cols)), 0, target))
    kept = min(HELD_BLOCKS, len(offsets))
    held_copies = []
    for i in range(kept):
        slot = mine - 1 - i

        def where(table_ref, slot=slot):
            return 0, pl.ds(pl.multiple_of(table_ref[slot] * own_cols, 128), own_cols)

        held_copies.append((0, where, i, (everything,)))
    early = [gain_slab, own_bias, *cosines, *sines, *masks]
    table, flags, weights = resident([table, flags], early, [q_weight, kv_weight], copies, [(slab, group * width)])
    _, *held = resident([table], [], [out_weight], held_copies, [(own_cols, slab)] * kept)
    held = {mine - 1 - i: w for i, w in enumerate(held)}
    mixing_weight = pltpu.with_memory_space_constraint(out_weight, pltpu.HBM)

    def flag(i):
        return flags[i : i + 1, :1] > 0.5

    def layer(own_rows, tick, earlier):
        pieces = [own_rows] + [around(own_rows, "gz", -j) for j in range(1, size_gz)]
        scaled, total, part = enter(table, 0, pieces, gain_slab, weights, width)
        received = []
        for k, o in enumerate(far_first):
            if k:
                part = project_block(table, k, scaled, weights, width, jnp.bfloat16)
            received.append(to_offset(part, *o))
        totals = [total]
        for o in far_first:
            totals.append(to_offset(total, *o))
        projected = project_block(table, mine, scaled, weights, width, jnp.float32)
        attended, keys, values = attend(
            projected,
            received,
            totals,
            own_bias,
            cosines[tick],
            sines[tick],
            masks[tick],
            earlier[: CHUNKS - 1],
            own_heads,
            used_heads,
            features,
        )
        seen = [(keys, values)] + earlier
        arrived = []
        for o in offsets:
            arrived.append(to_offset(attended, *o))
        (sums,) = mix_blocks(table, [mine], [attended], mixing_weight, held, None, 1)
        back = list(range(len(offsets), mine))
        if len(offsets) > 1:
            (sums,) = mix_blocks(table, back[:-1], arrived[:-1], mixing_weight, held, sums, 1)
        own_sum, *others = mix_blocks(table, back[-1:], arrived[-1:], mixing_weight, held, sums, size_gz)
        result = leave(own_rows, own_sum, [around(piece, "gz", j + 1) for j, piece in enumerate(others)])
        return result, seen

    results = []
    carried = None
    earlier = []
    for tick in range(ticks):
        if carried is None:
            current = entering[0]
        elif tick < jobs:
            current = jnp.where(flag(0), entering[tick], carried)
        else:
            current = carried
        result, earlier = layer(current, tick, earlier)
        results.append(result)
        if tick < ticks - 1:
            carried = lax.ppermute(result, "section", [(i, i + 1) for i in range(sections - 1)])

    stored = [sum_of([(flag(s), results[job + s]) for s in range(sections)]) for job in range(jobs)]
    return jnp.stack([collect(stored[m * CHUNKS : (m + 1) * CHUNKS]) for m in range(micro_count)])[None]


def solution(mesh):
    return jax.shard_map(
        body,
        mesh=mesh,
        in_specs=(
            P(None, "gy", ("gx", "gz")),
            P("section", "gx"),
            P("section", ("gx", "gy"), "gz"),
            P("section", None, ("gx", "gy"), "gz"),
            P("section", "gz"),
            P("section", None, "gz"),
            P("section", "gz", ("gx", "gy")),
        ),
        out_specs=P("section", None, "gy", ("gx", "gz")),
        check_vma=False,
    )
```

profile of v0, /device:TPU:0, one launch (start us, length us, event | category | flops | bytes accessed | tf_op | source)
XLA Modules:
  0.0 303.3 jit_solution(1778175921011836029)
XLA Ops:
  1.8 4.4 %collective-permute-start = (bf16[64,2048]{1,0:T(8,128)(2,1)S(1)}, bf16[64,2048]{1,0:T(8,128)(2,1)S(1)}, u32[]{:S(2)}, u32[]{:S(2)}) collective-permute-start(bf16[64,2048]{1,0:T(8,128)(2,1)S(1)} %get-tuple-element.104), channel_id=1, source_target_pairs={{0,1},{1,3},{2,0},{3,2},{4,5},{5,7},{6,4},{7,6},{8,9},{9,11},{10,8... | collective-permute-start | bytes 786440 | tf_op jit(solution)/shard_map/ppermute | solution.py:332
  13.3 7.8 %shard_map.73 = (s32[7]{0:T(128)S(4)}, f32[12,128]{1,0:T(8,128)S(1)}, bf16[2048,5120]{1,0:T(8,128)(2,1)S(1)}) custom-call(s32[7]{0:T(128)S(1)} %stack.61.refs_0_, f32[12,128]{1,0:T(8,128)S(1)} %broadcast_in_dim.87.refs_1_, bf16[1,2048,4096]{2,1,0:T(8,128)(2,1)} %refs_2_.1, bf16[1,2,2048,512]{3,2,1,0:T(8,128)(2,1)} %refs_3_.1, ...), custom_call_target="tpu_custom_call" | custom-call | flops 4294967296 | tf_op jit(solution)/shard_map/pallas_call | solution.py:52
  21.1 2.0 shard_map.74
  32.9 12.2 %collective-permute-done.8.refs_6_ = f32[8,128]{1,0:T(8,128)S(1)} collective-permute-done((f32[8,128]{1,0:T(8,128)S(1)}, f32[8,128]{1,0:T(8,128)S(1)}, u32[]{:S(2)}, u32[]{:S(2)}) %collective-permute-start.8) | collective-permute-done | bytes 4128 | tf_op jit(solution)/shard_map/ppermute | solution.py:315
  46.8 2.8 collective-permute-done.6.refs_4_
  49.6 2.3 shard_map.78
  52.9 2.6 collective-permute-start.9
  55.5 4.7 %shard_map.79 = (s32[7]{0:T(128)S(4)}, bf16[1024,2048]{1,0:T(8,128)(2,1)S(1)}, bf16[1024,2048]{1,0:T(8,128)(2,1)S(1)}, bf16[1024,2048]{1,0:T(8,128)(2,1)S(1)}) custom-call(s32[7]{0:T(128)S(4)} %get-tuple-element.50.table_ref.refs_0_, bf16[1,4096,2048]{2,1,0:T(8,128)(2,1)} %w_ref.29), custom_call_target="tpu_custom_call" | custom-call | flops 4294967296 | tf_op jit(solution)/shard_map/pallas_call | solution.py:52
  60.2 2.6 shard_map.80.refs_4_
  67.9 3.7 %collective-permute-start.13 = (bf16[64,2048]{1,0:T(8,128)(2,1)S(1)}, bf16[64,2048]{1,0:T(8,128)(2,1)S(1)}, u32[]{:S(2)}, u32[]{:S(2)}) collective-permute-start(bf16[64,2048]{1,0:T(8,128)(2,1)S(1)} %shard_map.83), channel_id=1, source_target_pairs={{0,8},{8,16},{16,24},{1,9},{9,17},{17,25},{2,10},{10,18},{18,26},{... | collective-permute-start | bytes 786440 | tf_op jit(solution)/shard_map/ppermute | solution.py:492
  72.8 4.4 %collective-permute-done.13 = bf16[64,2048]{1,0:T(8,128)(2,1)S(1)} collective-permute-done((bf16[64,2048]{1,0:T(8,128)(2,1)S(1)}, bf16[64,2048]{1,0:T(8,128)(2,1)S(1)}, u32[]{:S(2)}, u32[]{:S(2)}) %collective-permute-start.13) | collective-permute-done | bytes 262176 | tf_op jit(solution)/shard_map/ppermute | solution.py:492
  78.9 2.1 shard_map.84
  90.0 12.8 %collective-permute-done.20.refs_6_ = f32[8,128]{1,0:T(8,128)S(1)} collective-permute-done((f32[8,128]{1,0:T(8,128)S(1)}, f32[8,128]{1,0:T(8,128)S(1)}, u32[]{:S(2)}, u32[]{:S(2)}) %collective-permute-start.20) | collective-permute-done | bytes 4128 | tf_op jit(solution)/shard_map/ppermute | solution.py:315
  104.5 2.8 collective-permute-done.18.refs_4_
  109.3 2.8 collective-permute-start.21
  112.1 2.5 shard_map.89.refs_4_
  114.6 2.8 collective-permute-done.23.refs_1_
  117.4 2.9 collective-permute-done.22.refs_0_
  124.1 4.4 %collective-permute-start.25 = (bf16[64,2048]{1,0:T(8,128)(2,1)S(1)}, bf16[64,2048]{1,0:T(8,128)(2,1)S(1)}, u32[]{:S(2)}, u32[]{:S(2)}) collective-permute-start(bf16[64,2048]{1,0:T(8,128)(2,1)S(1)} %shard_map.92), channel_id=1, source_target_pairs={{0,8},{8,16},{16,24},{1,9},{9,17},{17,25},{2,10},{10,18},{18,26},{... | collective-permute-start | bytes 786440 | tf_op jit(solution)/shard_map/ppermute | solution.py:492
  128.5 5.8 %collective-permute-done.25.refs_0_.x_ref = bf16[64,2048]{1,0:T(8,128)(2,1)S(1)} collective-permute-done((bf16[64,2048]{1,0:T(8,128)(2,1)S(1)}, bf16[64,2048]{1,0:T(8,128)(2,1)S(1)}, u32[]{:S(2)}, u32[]{:S(2)}) %collective-permute-start.25) | collective-permute-done | bytes 262176 | tf_op jit(solution)/shard_map/ppermute | solution.py:492
  135.9 2.0 shard_map.93
  141.3 2.0 collective-permute-start.28
  146.9 13.0 %collective-permute-done.32.refs_6_ = f32[8,128]{1,0:T(8,128)S(1)} collective-permute-done((f32[8,128]{1,0:T(8,128)S(1)}, f32[8,128]{1,0:T(8,128)S(1)}, u32[]{:S(2)}, u32[]{:S(2)}) %collective-permute-start.32) | collective-permute-done | bytes 4128 | tf_op jit(solution)/shard_map/ppermute | solution.py:315
  161.6 2.8 collective-permute-done.30.refs_4_
  166.4 2.8 collective-permute-start.33
  169.1 2.5 shard_map.98.refs_4_
  171.7 2.8 collective-permute-done.35.refs_1_
  174.5 2.9 collective-permute-done.34.refs_0_
  181.2 4.7 %collective-permute-start.37 = (bf16[64,2048]{1,0:T(8,128)(2,1)S(1)}, bf16[64,2048]{1,0:T(8,128)(2,1)S(1)}, u32[]{:S(2)}, u32[]{:S(2)}) collective-permute-start(bf16[64,2048]{1,0:T(8,128)(2,1)S(1)} %shard_map.101), channel_id=1, source_target_pairs={{0,8},{8,16},{16,24},{1,9},{9,17},{17,25},{2,10},{10,18},{18,26},{... | collective-permute-start | bytes 786440 | tf_op jit(solution)/shard_map/ppermute | solution.py:492
  185.8 5.6 %collective-permute-done.37.refs_0_.x_ref = bf16[64,2048]{1,0:T(8,128)(2,1)S(1)} collective-permute-done((bf16[64,2048]{1,0:T(8,128)(2,1)S(1)}, bf16[64,2048]{1,0:T(8,128)(2,1)S(1)}, u32[]{:S(2)}, u32[]{:S(2)}) %collective-permute-start.37) | collective-permute-done | bytes 262176 | tf_op jit(solution)/shard_map/ppermute | solution.py:492
  193.0 2.1 shard_map.102
  203.9 13.0 %collective-permute-done.44.refs_6_ = f32[8,128]{1,0:T(8,128)S(1)} collective-permute-done((f32[8,128]{1,0:T(8,128)S(1)}, f32[8,128]{1,0:T(8,128)S(1)}, u32[]{:S(2)}, u32[]{:S(2)}) %collective-permute-start.44) | collective-permute-done | bytes 4128 | tf_op jit(solution)/shard_map/ppermute | solution.py:315
  218.7 2.8 collective-permute-done.42.refs_4_
  223.4 2.8 collective-permute-start.45
  226.2 2.5 shard_map.107.refs_4_
  228.7 2.8 collective-permute-done.47.refs_1_
  231.6 2.9 collective-permute-done.46.refs_0_
  238.2 4.4 %collective-permute-start.49 = (bf16[64,2048]{1,0:T(8,128)(2,1)S(1)}, bf16[64,2048]{1,0:T(8,128)(2,1)S(1)}, u32[]{:S(2)}, u32[]{:S(2)}) collective-permute-start(bf16[64,2048]{1,0:T(8,128)(2,1)S(1)} %shard_map.110), channel_id=1, source_target_pairs={{0,8},{8,16},{16,24},{1,9},{9,17},{17,25},{2,10},{10,18},{18,26},{... | collective-permute-start | bytes 786440 | tf_op jit(solution)/shard_map/ppermute | solution.py:492
  242.6 5.8 %collective-permute-done.49.refs_0_.x_ref = bf16[64,2048]{1,0:T(8,128)(2,1)S(1)} collective-permute-done((bf16[64,2048]{1,0:T(8,128)(2,1)S(1)}, bf16[64,2048]{1,0:T(8,128)(2,1)S(1)}, u32[]{:S(2)}, u32[]{:S(2)}) %collective-permute-start.49) | collective-permute-done | bytes 262176 | tf_op jit(solution)/shard_map/ppermute | solution.py:492
  250.0 2.1 shard_map.111
  255.5 2.0 collective-permute-start.52
  261.0 13.0 %collective-permute-done.56.refs_6_ = f32[8,128]{1,0:T(8,128)S(1)} collective-permute-done((f32[8,128]{1,0:T(8,128)S(1)}, f32[8,128]{1,0:T(8,128)S(1)}, u32[]{:S(2)}, u32[]{:S(2)}) %collective-permute-start.56) | collective-permute-done | bytes 4128 | tf_op jit(solution)/shard_map/ppermute | solution.py:315
  275.7 2.8 collective-permute-done.54.refs_4_
  280.9 2.8 collective-permute-start.57
  283.6 2.5 shard_map.116.refs_4_
  286.2 2.8 collective-permute-done.59.refs_1_
  289.0 2.8 collective-permute-done.58.refs_0_
  299.5 2.9 collective-permute-done.61
  (163 shorter events, 92.6 us)
Async XLA Ops:
  1.1 12.0 %collective-permute-start.1 = (bf16[64,2048]{1,0:T(8,128)(2,1)S(1)}, bf16[64,2048]{1,0:T(8,128)(2,1)S(1)}, u32[]{:S(2)}, u32[]{:S(2)}) collective-permute-start(bf16[64,2048]{1,0:T(8,128)(2,1)S(1)} %get-tuple-element.103), channel_id=1, source_target_pairs={{0,0},{1,2},{2,1},{3,3},{4,4},{5,6},{6,5},{7,7},{8,8},{9,10},{10,9... | collective-permute-start | bytes 786440 | tf_op jit(solution)/shard_map/ppermute | solution.py:332
  1.8 11.4 %collective-permute-start = (bf16[64,2048]{1,0:T(8,128)(2,1)S(1)}, bf16[64,2048]{1,0:T(8,128)(2,1)S(1)}, u32[]{:S(2)}, u32[]{:S(2)}) collective-permute-start(bf16[64,2048]{1,0:T(8,128)(2,1)S(1)} %get-tuple-element.104), channel_id=1, source_target_pairs={{0,1},{1,3},{2,0},{3,2},{4,5},{5,7},{6,4},{7,6},{8,9},{9,11},{10,8... | collective-permute-start | bytes 786440 | tf_op jit(solution)/shard_map/ppermute | solution.py:332
  13.2 7.9 %collective-permute-start.2 = (bf16[64,2048]{1,0:T(8,128)(2,1)S(1)}, bf16[64,2048]{1,0:T(8,128)(2,1)S(1)}, u32[]{:S(2)}, u32[]{:S(2)}) collective-permute-start(bf16[64,2048]{1,0:T(8,128)(2,1)S(1)} %broadcast_select_fusion.2.refs_0_.x_ref), channel_id=1, source_target_pairs={{0,1},{1,0},{2,3},{3,2},{4,5},{5,4},{6,7},{7,6},{8,9},{9,8},{10,11... | collective-permute-start | bytes 786440 | tf_op jit(solution)/shard_map/ppermute | solution.py:266
  26.6 23.0 %collective-permute-start.4 = (bf16[128,1280]{1,0:T(8,128)(2,1)S(1)}, bf16[128,1280]{1,0:T(8,128)(2,1)S(1)}, u32[]{:S(2)}, u32[]{:S(2)}) collective-permute-start(bf16[128,1280]{1,0:T(8,128)(2,1)S(1)} %shard_map.76), channel_id=1, source_target_pairs={{0,4},{2,6},{4,0},{6,2},{1,5},{3,7},{5,1},{7,3},{8,12},{10,14},{12... | collective-permute-start | bytes 983048 | tf_op jit(solution)/shard_map/ppermute | solution.py:315
  28.1 21.5 %collective-permute-start.5 = (bf16[128,1280]{1,0:T(8,128)(2,1)S(1)}, bf16[128,1280]{1,0:T(8,128)(2,1)S(1)}, u32[]{:S(2)}, u32[]{:S(2)}) collective-permute-start(bf16[128,1280]{1,0:T(8,128)(2,1)S(1)} %shard_map.77), channel_id=1, source_target_pairs={{0,2},{2,0},{4,6},{6,4},{1,3},{3,1},{5,7},{7,5},{8,10},{10,8},{12,... | collective-permute-start | bytes 983048 | tf_op jit(solution)/shard_map/ppermute | solution.py:315
  29.4 20.2 %collective-permute-start.3 = (bf16[128,1280]{1,0:T(8,128)(2,1)S(1)}, bf16[128,1280]{1,0:T(8,128)(2,1)S(1)}, u32[]{:S(2)}, u32[]{:S(2)}) collective-permute-start(bf16[128,1280]{1,0:T(8,128)(2,1)S(1)} %get-tuple-element.53), channel_id=1, source_target_pairs={{0,6},{2,4},{4,2},{6,0},{1,7},{3,5},{5,3},{7,1},{8,14},{10,12},{12... | collective-permute-start | bytes 983048 | tf_op jit(solution)/shard_map/ppermute | solution.py:315
  30.2 14.9 %collective-permute-start.8 = (f32[8,128]{1,0:T(8,128)S(1)}, f32[8,128]{1,0:T(8,128)S(1)}, u32[]{:S(2)}, u32[]{:S(2)}) collective-permute-start(f32[8,128]{1,0:T(8,128)S(1)} %get-tuple-element.54.refs_3_), channel_id=1, source_target_pairs={{0,2},{2,0},{4,6},{6,4},{1,3},{3,1},{5,7},{7,5},{8,10},{10,8},{12,... | collective-permute-start | bytes 12296 | tf_op jit(solution)/shard_map/ppermute | solution.py:315
  31.4 15.4 %collective-permute-start.7 = (f32[8,128]{1,0:T(8,128)S(1)}, f32[8,128]{1,0:T(8,128)S(1)}, u32[]{:S(2)}, u32[]{:S(2)}) collective-permute-start(f32[8,128]{1,0:T(8,128)S(1)} %get-tuple-element.54.refs_3_), channel_id=1, source_target_pairs={{0,4},{2,6},{4,0},{6,2},{1,5},{3,7},{5,1},{7,3},{8,12},{10,14},{12... | collective-permute-start | bytes 12296 | tf_op jit(solution)/shard_map/ppermute | solution.py:315
  51.9 10.8 %collective-permute-start.11 = (bf16[128,1024]{1,0:T(8,128)(2,1)S(1)}, bf16[128,1024]{1,0:T(8,128)(2,1)S(1)}, u32[]{:S(2)}, u32[]{:S(2)}) collective-permute-start(bf16[128,1024]{1,0:T(8,128)(2,1)S(1)} %get-tuple-element.55.refs_0_), channel_id=1, source_target_pairs={{0,4},{2,6},{4,0},{6,2},{1,5},{3,7},{5,1},{7,3},{8,12},{10,14},{12... | collective-permute-start | bytes 786440 | tf_op jit(solution)/shard_map/ppermute | solution.py:315
  52.6 11.5 %collective-permute-start.10 = (bf16[128,1024]{1,0:T(8,128)(2,1)S(1)}, bf16[128,1024]{1,0:T(8,128)(2,1)S(1)}, u32[]{:S(2)}, u32[]{:S(2)}) collective-permute-start(bf16[128,1024]{1,0:T(8,128)(2,1)S(1)} %get-tuple-element.55.refs_0_), channel_id=1, source_target_pairs={{0,2},{2,0},{4,6},{6,4},{1,3},{3,1},{5,7},{7,5},{8,10},{10,8},{12,... | collective-permute-start | bytes 786440 | tf_op jit(solution)/shard_map/ppermute | solution.py:315
  52.9 12.6 %collective-permute-start.9 = (bf16[128,1024]{1,0:T(8,128)(2,1)S(1)}, bf16[128,1024]{1,0:T(8,128)(2,1)S(1)}, u32[]{:S(2)}, u32[]{:S(2)}) collective-permute-start(bf16[128,1024]{1,0:T(8,128)(2,1)S(1)} %get-tuple-element.55.refs_0_), channel_id=1, source_target_pairs={{0,6},{2,4},{4,2},{6,0},{1,7},{3,5},{5,3},{7,1},{8,14},{10,12},{12... | collective-permute-start | bytes 786440 | tf_op jit(solution)/shard_map/ppermute | solution.py:315
  67.9 9.3 %collective-permute-start.13 = (bf16[64,2048]{1,0:T(8,128)(2,1)S(1)}, bf16[64,2048]{1,0:T(8,128)(2,1)S(1)}, u32[]{:S(2)}, u32[]{:S(2)}) collective-permute-start(bf16[64,2048]{1,0:T(8,128)(2,1)S(1)} %shard_map.83), channel_id=1, source_target_pairs={{0,8},{8,16},{16,24},{1,9},{9,17},{17,25},{2,10},{10,18},{18,26},{... | collective-permute-start | bytes 786440 | tf_op jit(solution)/shard_map/ppermute | solution.py:492
  84.4 23.0 %collective-permute-start.16 = (bf16[128,1280]{1,0:T(8,128)(2,1)S(1)}, bf16[128,1280]{1,0:T(8,128)(2,1)S(1)}, u32[]{:S(2)}, u32[]{:S(2)}) collective-permute-start(bf16[128,1280]{1,0:T(8,128)(2,1)S(1)} %shard_map.86), channel_id=1, source_target_pairs={{0,4},{2,6},{4,0},{6,2},{1,5},{3,7},{5,1},{7,3},{8,12},{10,14},{12... | collective-permute-start | bytes 983048 | tf_op jit(solution)/shard_map/ppermute | solution.py:315
  86.2 21.1 %collective-permute-start.17 = (bf16[128,1280]{1,0:T(8,128)(2,1)S(1)}, bf16[128,1280]{1,0:T(8,128)(2,1)S(1)}, u32[]{:S(2)}, u32[]{:S(2)}) collective-permute-start(bf16[128,1280]{1,0:T(8,128)(2,1)S(1)} %shard_map.87), channel_id=1, source_target_pairs={{0,2},{2,0},{4,6},{6,4},{1,3},{3,1},{5,7},{7,5},{8,10},{10,8},{12,... | collective-permute-start | bytes 983048 | tf_op jit(solution)/shard_map/ppermute | solution.py:315
  86.5 20.9 %collective-permute-start.15 = (bf16[128,1280]{1,0:T(8,128)(2,1)S(1)}, bf16[128,1280]{1,0:T(8,128)(2,1)S(1)}, u32[]{:S(2)}, u32[]{:S(2)}) collective-permute-start(bf16[128,1280]{1,0:T(8,128)(2,1)S(1)} %get-tuple-element.62), channel_id=1, source_target_pairs={{0,6},{2,4},{4,2},{6,0},{1,7},{3,5},{5,3},{7,1},{8,14},{10,12},{12... | collective-permute-start | bytes 983048 | tf_op jit(solution)/shard_map/ppermute | solution.py:315
  87.9 14.9 %collective-permute-start.20 = (f32[8,128]{1,0:T(8,128)S(1)}, f32[8,128]{1,0:T(8,128)S(1)}, u32[]{:S(2)}, u32[]{:S(2)}) collective-permute-start(f32[8,128]{1,0:T(8,128)S(1)} %get-tuple-element.63.refs_3_), channel_id=1, source_target_pairs={{0,2},{2,0},{4,6},{6,4},{1,3},{3,1},{5,7},{7,5},{8,10},{10,8},{12,... | collective-permute-start | bytes 12296 | tf_op jit(solution)/shard_map/ppermute | solution.py:315
  88.3 16.2 %collective-permute-start.19 = (f32[8,128]{1,0:T(8,128)S(1)}, f32[8,128]{1,0:T(8,128)S(1)}, u32[]{:S(2)}, u32[]{:S(2)}) collective-permute-start(f32[8,128]{1,0:T(8,128)S(1)} %get-tuple-element.63.refs_3_), channel_id=1, source_target_pairs={{0,4},{2,6},{4,0},{6,2},{1,5},{3,7},{5,1},{7,3},{8,12},{10,14},{12... | collective-permute-start | bytes 12296 | tf_op jit(solution)/shard_map/ppermute | solution.py:315
  108.5 8.9 %collective-permute-start.23 = (bf16[128,1024]{1,0:T(8,128)(2,1)S(1)}, bf16[128,1024]{1,0:T(8,128)(2,1)S(1)}, u32[]{:S(2)}, u32[]{:S(2)}) collective-permute-start(bf16[128,1024]{1,0:T(8,128)(2,1)S(1)} %get-tuple-element.66.refs_0_), channel_id=1, source_target_pairs={{0,4},{2,6},{4,0},{6,2},{1,5},{3,7},{5,1},{7,3},{8,12},{10,14},{12... | collective-permute-start | bytes 786440 | tf_op jit(solution)/shard_map/ppermute | solution.py:315
  108.9 11.4 %collective-permute-start.22 = (bf16[128,1024]{1,0:T(8,128)(2,1)S(1)}, bf16[128,1024]{1,0:T(8,128)(2,1)S(1)}, u32[]{:S(2)}, u32[]{:S(2)}) collective-permute-start(bf16[128,1024]{1,0:T(8,128)(2,1)S(1)} %get-tuple-element.66.refs_0_), channel_id=1, source_target_pairs={{0,2},{2,0},{4,6},{6,4},{1,3},{3,1},{5,7},{7,5},{8,10},{10,8},{12,... | collective-permute-start | bytes 786440 | tf_op jit(solution)/shard_map/ppermute | solution.py:315
  109.3 12.4 %collective-permute-start.21 = (bf16[128,1024]{1,0:T(8,128)(2,1)S(1)}, bf16[128,1024]{1,0:T(8,128)(2,1)S(1)}, u32[]{:S(2)}, u32[]{:S(2)}) collective-permute-start(bf16[128,1024]{1,0:T(8,128)(2,1)S(1)} %get-tuple-element.66.refs_0_), channel_id=1, source_target_pairs={{0,6},{2,4},{4,2},{6,0},{1,7},{3,5},{5,3},{7,1},{8,14},{10,12},{12... | collective-permute-start | bytes 786440 | tf_op jit(solution)/shard_map/ppermute | solution.py:315
  124.1 10.2 %collective-permute-start.25 = (bf16[64,2048]{1,0:T(8,128)(2,1)S(1)}, bf16[64,2048]{1,0:T(8,128)(2,1)S(1)}, u32[]{:S(2)}, u32[]{:S(2)}) collective-permute-start(bf16[64,2048]{1,0:T(8,128)(2,1)S(1)} %shard_map.92), channel_id=1, source_target_pairs={{0,8},{8,16},{16,24},{1,9},{9,17},{17,25},{2,10},{10,18},{18,26},{... | collective-permute-start | bytes 786440 | tf_op jit(solution)/shard_map/ppermute | solution.py:492
  141.3 23.1 %collective-permute-start.28 = (bf16[128,1280]{1,0:T(8,128)(2,1)S(1)}, bf16[128,1280]{1,0:T(8,128)(2,1)S(1)}, u32[]{:S(2)}, u32[]{:S(2)}) collective-permute-start(bf16[128,1280]{1,0:T(8,128)(2,1)S(1)} %shard_map.95), channel_id=1, source_target_pairs={{0,4},{2,6},{4,0},{6,2},{1,5},{3,7},{5,1},{7,3},{8,12},{10,14},{12... | collective-permute-start | bytes 983048 | tf_op jit(solution)/shard_map/ppermute | solution.py:315
  143.3 21.1 %collective-permute-start.29 = (bf16[128,1280]{1,0:T(8,128)(2,1)S(1)}, bf16[128,1280]{1,0:T(8,128)(2,1)S(1)}, u32[]{:S(2)}, u32[]{:S(2)}) collective-permute-start(bf16[128,1280]{1,0:T(8,128)(2,1)S(1)} %shard_map.96), channel_id=1, source_target_pairs={{0,2},{2,0},{4,6},{6,4},{1,3},{3,1},{5,7},{7,5},{8,10},{10,8},{12,... | collective-permute-start | bytes 983048 | tf_op jit(solution)/shard_map/ppermute | solution.py:315
  143.4 21.0 %collective-permute-start.27 = (bf16[128,1280]{1,0:T(8,128)(2,1)S(1)}, bf16[128,1280]{1,0:T(8,128)(2,1)S(1)}, u32[]{:S(2)}, u32[]{:S(2)}) collective-permute-start(bf16[128,1280]{1,0:T(8,128)(2,1)S(1)} %get-tuple-element.70), channel_id=1, source_target_pairs={{0,6},{2,4},{4,2},{6,0},{1,7},{3,5},{5,3},{7,1},{8,14},{10,12},{12... | collective-permute-start | bytes 983048 | tf_op jit(solution)/shard_map/ppermute | solution.py:315
  144.9 15.0 %collective-permute-start.32 = (f32[8,128]{1,0:T(8,128)S(1)}, f32[8,128]{1,0:T(8,128)S(1)}, u32[]{:S(2)}, u32[]{:S(2)}) collective-permute-start(f32[8,128]{1,0:T(8,128)S(1)} %get-tuple-element.71.refs_3_), channel_id=1, source_target_pairs={{0,2},{2,0},{4,6},{6,4},{1,3},{3,1},{5,7},{7,5},{8,10},{10,8},{12,... | collective-permute-start | bytes 12296 | tf_op jit(solution)/shard_map/ppermute | solution.py:315
  145.3 16.3 %collective-permute-start.31 = (f32[8,128]{1,0:T(8,128)S(1)}, f32[8,128]{1,0:T(8,128)S(1)}, u32[]{:S(2)}, u32[]{:S(2)}) collective-permute-start(f32[8,128]{1,0:T(8,128)S(1)} %get-tuple-element.71.refs_3_), channel_id=1, source_target_pairs={{0,4},{2,6},{4,0},{6,2},{1,5},{3,7},{5,1},{7,3},{8,12},{10,14},{12... | collective-permute-start | bytes 12296 | tf_op jit(solution)/shard_map/ppermute | solution.py:315
  165.6 8.9 %collective-permute-start.35 = (bf16[128,1024]{1,0:T(8,128)(2,1)S(1)}, bf16[128,1024]{1,0:T(8,128)(2,1)S(1)}, u32[]{:S(2)}, u32[]{:S(2)}) collective-permute-start(bf16[128,1024]{1,0:T(8,128)(2,1)S(1)} %get-tuple-element.74.refs_0_), channel_id=1, source_target_pairs={{0,4},{2,6},{4,0},{6,2},{1,5},{3,7},{5,1},{7,3},{8,12},{10,14},{12... | collective-permute-start | bytes 786440 | tf_op jit(solution)/shard_map/ppermute | solution.py:315
  166.0 11.4 %collective-permute-start.34 = (bf16[128,1024]{1,0:T(8,128)(2,1)S(1)}, bf16[128,1024]{1,0:T(8,128)(2,1)S(1)}, u32[]{:S(2)}, u32[]{:S(2)}) collective-permute-start(bf16[128,1024]{1,0:T(8,128)(2,1)S(1)} %get-tuple-element.74.refs_0_), channel_id=1, source_target_pairs={{0,2},{2,0},{4,6},{6,4},{1,3},{3,1},{5,7},{7,5},{8,10},{10,8},{12,... | collective-permute-start | bytes 786440 | tf_op jit(solution)/shard_map/ppermute | solution.py:315
  166.4 12.4 %collective-permute-start.33 = (bf16[128,1024]{1,0:T(8,128)(2,1)S(1)}, bf16[128,1024]{1,0:T(8,128)(2,1)S(1)}, u32[]{:S(2)}, u32[]{:S(2)}) collective-permute-start(bf16[128,1024]{1,0:T(8,128)(2,1)S(1)} %get-tuple-element.74.refs_0_), channel_id=1, source_target_pairs={{0,6},{2,4},{4,2},{6,0},{1,7},{3,5},{5,3},{7,1},{8,14},{10,12},{12... | collective-permute-start | bytes 786440 | tf_op jit(solution)/shard_map/ppermute | solution.py:315
  181.2 10.3 %collective-permute-start.37 = (bf16[64,2048]{1,0:T(8,128)(2,1)S(1)}, bf16[64,2048]{1,0:T(8,128)(2,1)S(1)}, u32[]{:S(2)}, u32[]{:S(2)}) collective-permute-start(bf16[64,2048]{1,0:T(8,128)(2,1)S(1)} %shard_map.101), channel_id=1, source_target_pairs={{0,8},{8,16},{16,24},{1,9},{9,17},{17,25},{2,10},{10,18},{18,26},{... | collective-permute-start | bytes 786440 | tf_op jit(solution)/shard_map/ppermute | solution.py:492
  198.4 23.0 %collective-permute-start.40 = (bf16[128,1280]{1,0:T(8,128)(2,1)S(1)}, bf16[128,1280]{1,0:T(8,128)(2,1)S(1)}, u32[]{:S(2)}, u32[]{:S(2)}) collective-permute-start(bf16[128,1280]{1,0:T(8,128)(2,1)S(1)} %shard_map.104), channel_id=1, source_target_pairs={{0,4},{2,6},{4,0},{6,2},{1,5},{3,7},{5,1},{7,3},{8,12},{10,14},{12... | collective-permute-start | bytes 983048 | tf_op jit(solution)/shard_map/ppermute | solution.py:315
  200.4 21.1 %collective-permute-start.41 = (bf16[128,1280]{1,0:T(8,128)(2,1)S(1)}, bf16[128,1280]{1,0:T(8,128)(2,1)S(1)}, u32[]{:S(2)}, u32[]{:S(2)}) collective-permute-start(bf16[128,1280]{1,0:T(8,128)(2,1)S(1)} %shard_map.105), channel_id=1, source_target_pairs={{0,2},{2,0},{4,6},{6,4},{1,3},{3,1},{5,7},{7,5},{8,10},{10,8},{12,... | collective-permute-start | bytes 983048 | tf_op jit(solution)/shard_map/ppermute | solution.py:315
  200.4 21.0 %collective-permute-start.39 = (bf16[128,1280]{1,0:T(8,128)(2,1)S(1)}, bf16[128,1280]{1,0:T(8,128)(2,1)S(1)}, u32[]{:S(2)}, u32[]{:S(2)}) collective-permute-start(bf16[128,1280]{1,0:T(8,128)(2,1)S(1)} %get-tuple-element.78), channel_id=1, source_target_pairs={{0,6},{2,4},{4,2},{6,0},{1,7},{3,5},{5,3},{7,1},{8,14},{10,12},{12... | collective-permute-start | bytes 983048 | tf_op jit(solution)/shard_map/ppermute | solution.py:315
  202.0 15.0 %collective-permute-start.44 = (f32[8,128]{1,0:T(8,128)S(1)}, f32[8,128]{1,0:T(8,128)S(1)}, u32[]{:S(2)}, u32[]{:S(2)}) collective-permute-start(f32[8,128]{1,0:T(8,128)S(1)} %get-tuple-element.79.refs_3_), channel_id=1, source_target_pairs={{0,2},{2,0},{4,6},{6,4},{1,3},{3,1},{5,7},{7,5},{8,10},{10,8},{12,... | collective-permute-start | bytes 12296 | tf_op jit(solution)/shard_map/ppermute | solution.py:315
  202.4 16.3 %collective-permute-start.43 = (f32[8,128]{1,0:T(8,128)S(1)}, f32[8,128]{1,0:T(8,128)S(1)}, u32[]{:S(2)}, u32[]{:S(2)}) collective-permute-start(f32[8,128]{1,0:T(8,128)S(1)} %get-tuple-element.79.refs_3_), channel_id=1, source_target_pairs={{0,4},{2,6},{4,0},{6,2},{1,5},{3,7},{5,1},{7,3},{8,12},{10,14},{12... | collective-permute-start | bytes 12296 | tf_op jit(solution)/shard_map/ppermute | solution.py:315
  222.6 8.9 %collective-permute-start.47 = (bf16[128,1024]{1,0:T(8,128)(2,1)S(1)}, bf16[128,1024]{1,0:T(8,128)(2,1)S(1)}, u32[]{:S(2)}, u32[]{:S(2)}) collective-permute-start(bf16[128,1024]{1,0:T(8,128)(2,1)S(1)} %get-tuple-element.82.refs_0_), channel_id=1, source_target_pairs={{0,4},{2,6},{4,0},{6,2},{1,5},{3,7},{5,1},{7,3},{8,12},{10,14},{12... | collective-permute-start | bytes 786440 | tf_op jit(solution)/shard_map/ppermute | solution.py:315
  223.1 11.4 %collective-permute-start.46 = (bf16[128,1024]{1,0:T(8,128)(2,1)S(1)}, bf16[128,1024]{1,0:T(8,128)(2,1)S(1)}, u32[]{:S(2)}, u32[]{:S(2)}) collective-permute-start(bf16[128,1024]{1,0:T(8,128)(2,1)S(1)} %get-tuple-element.82.refs_0_), channel_id=1, source_target_pairs={{0,2},{2,0},{4,6},{6,4},{1,3},{3,1},{5,7},{7,5},{8,10},{10,8},{12,... | collective-permute-start | bytes 786440 | tf_op jit(solution)/shard_map/ppermute | solution.py:315
  223.4 12.4 %collective-permute-start.45 = (bf16[128,1024]{1,0:T(8,128)(2,1)S(1)}, bf16[128,1024]{1,0:T(8,128)(2,1)S(1)}, u32[]{:S(2)}, u32[]{:S(2)}) collective-permute-start(bf16[128,1024]{1,0:T(8,128)(2,1)S(1)} %get-tuple-element.82.refs_0_), channel_id=1, source_target_pairs={{0,6},{2,4},{4,2},{6,0},{1,7},{3,5},{5,3},{7,1},{8,14},{10,12},{12... | collective-permute-start | bytes 786440 | tf_op jit(solution)/shard_map/ppermute | solution.py:315
  238.2 10.2 %collective-permute-start.49 = (bf16[64,2048]{1,0:T(8,128)(2,1)S(1)}, bf16[64,2048]{1,0:T(8,128)(2,1)S(1)}, u32[]{:S(2)}, u32[]{:S(2)}) collective-permute-start(bf16[64,2048]{1,0:T(8,128)(2,1)S(1)} %shard_map.110), channel_id=1, source_target_pairs={{0,8},{8,16},{16,24},{1,9},{9,17},{17,25},{2,10},{10,18},{18,26},{... | collective-permute-start | bytes 786440 | tf_op jit(solution)/shard_map/ppermute | solution.py:492
  255.5 23.1 %collective-permute-start.52 = (bf16[128,1280]{1,0:T(8,128)(2,1)S(1)}, bf16[128,1280]{1,0:T(8,128)(2,1)S(1)}, u32[]{:S(2)}, u32[]{:S(2)}) collective-permute-start(bf16[128,1280]{1,0:T(8,128)(2,1)S(1)} %shard_map.113), channel_id=1, source_target_pairs={{0,4},{2,6},{4,0},{6,2},{1,5},{3,7},{5,1},{7,3},{8,12},{10,14},{12... | collective-permute-start | bytes 983048 | tf_op jit(solution)/shard_map/ppermute | solution.py:315
  257.4 21.1 %collective-permute-start.53 = (bf16[128,1280]{1,0:T(8,128)(2,1)S(1)}, bf16[128,1280]{1,0:T(8,128)(2,1)S(1)}, u32[]{:S(2)}, u32[]{:S(2)}) collective-permute-start(bf16[128,1280]{1,0:T(8,128)(2,1)S(1)} %shard_map.114), channel_id=1, source_target_pairs={{0,2},{2,0},{4,6},{6,4},{1,3},{3,1},{5,7},{7,5},{8,10},{10,8},{12,... | collective-permute-start | bytes 983048 | tf_op jit(solution)/shard_map/ppermute | solution.py:315
  257.5 21.0 %collective-permute-start.51 = (bf16[128,1280]{1,0:T(8,128)(2,1)S(1)}, bf16[128,1280]{1,0:T(8,128)(2,1)S(1)}, u32[]{:S(2)}, u32[]{:S(2)}) collective-permute-start(bf16[128,1280]{1,0:T(8,128)(2,1)S(1)} %get-tuple-element.86), channel_id=1, source_target_pairs={{0,6},{2,4},{4,2},{6,0},{1,7},{3,5},{5,3},{7,1},{8,14},{10,12},{12... | collective-permute-start | bytes 983048 | tf_op jit(solution)/shard_map/ppermute | solution.py:315
  259.0 15.0 %collective-permute-start.56 = (f32[8,128]{1,0:T(8,128)S(1)}, f32[8,128]{1,0:T(8,128)S(1)}, u32[]{:S(2)}, u32[]{:S(2)}) collective-permute-start(f32[8,128]{1,0:T(8,128)S(1)} %get-tuple-element.87.refs_3_), channel_id=1, source_target_pairs={{0,2},{2,0},{4,6},{6,4},{1,3},{3,1},{5,7},{7,5},{8,10},{10,8},{12,... | collective-permute-start | bytes 12296 | tf_op jit(solution)/shard_map/ppermute | solution.py:315
  259.5 16.2 %collective-permute-start.55 = (f32[8,128]{1,0:T(8,128)S(1)}, f32[8,128]{1,0:T(8,128)S(1)}, u32[]{:S(2)}, u32[]{:S(2)}) collective-permute-start(f32[8,128]{1,0:T(8,128)S(1)} %get-tuple-element.87.refs_3_), channel_id=1, source_target_pairs={{0,4},{2,6},{4,0},{6,2},{1,5},{3,7},{5,1},{7,3},{8,12},{10,14},{12... | collective-permute-start | bytes 12296 | tf_op jit(solution)/shard_map/ppermute | solution.py:315
  280.1 8.9 %collective-permute-start.59 = (bf16[128,1024]{1,0:T(8,128)(2,1)S(1)}, bf16[128,1024]{1,0:T(8,128)(2,1)S(1)}, u32[]{:S(2)}, u32[]{:S(2)}) collective-permute-start(bf16[128,1024]{1,0:T(8,128)(2,1)S(1)} %get-tuple-element.90.refs_0_), channel_id=1, source_target_pairs={{0,4},{2,6},{4,0},{6,2},{1,5},{3,7},{5,1},{7,3},{8,12},{10,14},{12... | collective-permute-start | bytes 786440 | tf_op jit(solution)/shard_map/ppermute | solution.py:315
  280.5 11.3 %collective-permute-start.58 = (bf16[128,1024]{1,0:T(8,128)(2,1)S(1)}, bf16[128,1024]{1,0:T(8,128)(2,1)S(1)}, u32[]{:S(2)}, u32[]{:S(2)}) collective-permute-start(bf16[128,1024]{1,0:T(8,128)(2,1)S(1)} %get-tuple-element.90.refs_0_), channel_id=1, source_target_pairs={{0,2},{2,0},{4,6},{6,4},{1,3},{3,1},{5,7},{7,5},{8,10},{10,8},{12,... | collective-permute-start | bytes 786440 | tf_op jit(solution)/shard_map/ppermute | solution.py:315
  280.9 12.3 %collective-permute-start.57 = (bf16[128,1024]{1,0:T(8,128)(2,1)S(1)}, bf16[128,1024]{1,0:T(8,128)(2,1)S(1)}, u32[]{:S(2)}, u32[]{:S(2)}) collective-permute-start(bf16[128,1024]{1,0:T(8,128)(2,1)S(1)} %get-tuple-element.90.refs_0_), channel_id=1, source_target_pairs={{0,6},{2,4},{4,2},{6,0},{1,7},{3,5},{5,3},{7,1},{8,14},{10,12},{12... | collective-permute-start | bytes 786440 | tf_op jit(solution)/shard_map/ppermute | solution.py:315
  297.4 5.0 %collective-permute-start.61 = (bf16[64,2048]{1,0:T(8,128)(2,1)S(1)}, bf16[64,2048]{1,0:T(8,128)(2,1)S(1)}, u32[]{:S(2)}, u32[]{:S(2)}) collective-permute-start(bf16[64,2048]{1,0:T(8,128)(2,1)S(1)} %broadcast_select_fusion.3), channel_id=1, source_target_pairs={{0,2},{1,0},{2,3},{3,1},{4,6},{5,4},{6,7},{7,5},{8,10},{9,8},{10,1... | collective-permute-start | bytes 786440 | tf_op jit(solution)/shard_map/ppermute | solution.py:345
  (19 other events, 80.0 us)
where the time goes:
time: 307 us; the launch traced here: 303 us
  waiting for transfers between devices  139 us (45%)
  Pallas kernels  78.9 us (26%)
  starting transfers between devices  69.6 us (23%)
  between operations  8.44 us (3%)
  local copies, waits for them, and re-layouts  4.23 us (1%)
    ppermute x45, waiting for transfers between devices, to_offset(): return lax.ppermute(value, ('gx', 'gy'), pairs)  102 us
    ppermute x45, starting transfers between devices, to_offset(): return lax.ppermute(value, ('gx', 'gy'), pairs)  46.1 us
    pallas_call x15, Pallas kernels, project_block(): pl.pallas_call(kernel, out_shape=jax.ShapeDtypeStruct((rows.shape[0], wid...  25.3 us
    pallas_call x15, Pallas kernels, mix_blocks(): pl.pallas_call(kernel, out_shape=[jax.ShapeDtypeStruct((share, slab), jnp...  23.1 us
    ppermute x4, waiting for transfers between devices, body(): lax.ppermute(result, 'section', [(i, i + 1) for i in range(sections - 1)])  21.7 us
    ppermute x4, starting transfers between devices, body(): lax.ppermute(result, 'section', [(i, i + 1) for i in range(sections - 1)])  17.1 us
    pallas_call x2, Pallas kernels, resident(): pl.pallas_call(kernel, out_shape=[(pltpu.SMEM if v.dtype == jnp.int32 els...  12.5 us
    ppermute x10, waiting for transfers between devices, around(): lax.ppermute(value, axis, [(i, (i + steps) % count) for i in range(count)])  12.2 us
  transfers between devices with their start and end apart: 63, of which 33 were waited for; matrix products, arithmetic and copies ran while one was open for 2% of the time, Pallas kernels for 13%

commit v1 on v0

--- a/solution.py
+++ b/solution.py
@@ -10,6 +10,7 @@
 EPSILON = 1e-06
 NEG_FILL = -1e30
 CHUNKS = 2
+TAIL = 8
 HELD_BLOCKS = 3
 WHOLE = pl.BlockSpec(memory_space=pltpu.VMEM)
 SCALARS = pl.BlockSpec(memory_space=pltpu.SMEM)
@@ -62,59 +63,84 @@
     )(*small, *[pltpu.with_memory_space_constraint(x, pltpu.HBM) for x in sources], *early)
 
 
-def project_into(o_ref, x_ref, w_ref, start, width):
+def project_into(refs, x_ref, w_ref, start, width):
     tile = tile_of(width)
+    rows = x_ref.shape[0] // len(refs)
 
     def step(i, _):
-        o_ref[:, pl.ds(pl.multiple_of(i * tile, 128), tile)] = jnp.dot(
+        spot = pl.ds(pl.multiple_of(i * tile, 128), tile)
+        out = jnp.dot(
             x_ref[...],
             w_ref[:, pl.ds(pl.multiple_of(start + i * tile, 128), tile)],
             preferred_element_type=jnp.float32,
-        ).astype(o_ref.dtype)
+        )
+        for h, ref in enumerate(refs):
+            ref[:rows, spot] = out[h * rows : (h + 1) * rows].astype(ref.dtype)
         return 0
 
     lax.fori_loop(0, width // tile, step, 0)
 
 
-def project_block(table, slot, rows, weight, width, kind):
-    def kernel(table_ref, x_ref, w_ref, o_ref):
-        project_into(o_ref, x_ref, w_ref, table_ref[slot] * width, width)
-
-    return pl.pallas_call(
-        kernel,
-        out_shape=jax.ShapeDtypeStruct((rows.shape[0], width), kind),
+def project_block(table, slot, rows, weight, width, kind, pieces=1):
+    def kernel(table_ref, x_ref, w_ref, *refs):
+        project_into(refs, x_ref, w_ref, table_ref[slot] * width, width)
+
+    return pl.pallas_call(
+        kernel,
+        out_shape=[jax.ShapeDtypeStruct((rows.shape[0] // pieces, width), kind)] * pieces,
         in_specs=[SCALARS, WHOLE, WHOLE],
-        out_specs=WHOLE,
+        out_specs=[WHOLE] * pieces,
         compiler_params=LIMIT,
         cost_estimate=effort(2 * rows.shape[0] * rows.shape[1] * width),
     )(table, rows, weight)
 
 
-def enter(table, slot, pieces, gain, weight, width):
+def write_split(ref, start, row):
+    upper = row.astype(jnp.bfloat16)
+    rest = row - upper.astype(jnp.float32)
+    middle = rest.astype(jnp.bfloat16)
+    lower = (rest - middle.astype(jnp.float32)).astype(jnp.bfloat16)
+    zero = jnp.zeros((TAIL - 3, row.shape[1]), jnp.bfloat16)
+    ref[start:, : row.shape[1]] = jnp.concatenate([upper, middle, lower, zero], axis=0)
+    if ref.shape[1] > row.shape[1]:
+        ref[start:, row.shape[1] :] = jnp.zeros((TAIL, ref.shape[1] - row.shape[1]), jnp.bfloat16)
+
+
+def read_split(ref, start, size):
+    value = ref[start : start + TAIL, :size].astype(jnp.float32)
+    return value[0:1] + value[1:2] + value[2:3]
+
+
+def enter(table, slot, pieces, gain, weight, width, halves):
     count = len(pieces)
     share, slab = pieces[0].shape
     chunk = share * count
+    half = chunk // halves
+    tail = TAIL if halves > 1 else 0
 
     def kernel(table_ref, gain_ref, w_ref, *refs):
-        scaled_ref, total_ref, o_ref = refs[count:]
+        scaled_ref, total_ref, *o_refs = refs[count:]
         totals = []
         for i in range(count):
             wide = refs[i][...].astype(jnp.float32)
             scaled_ref[i * share : (i + 1) * share, :] = (wide * gain_ref[...]).astype(jnp.bfloat16)
             totals.append(jnp.sum(wide * wide, axis=1, keepdims=True))
         total = jnp.broadcast_to(jnp.concatenate(totals, axis=0), (chunk, 128))
-        total_ref[...] = jnp.transpose(total)[:8]
-        project_into(o_ref, scaled_ref, w_ref, table_ref[slot] * width, width)
-
-    return pl.pallas_call(
-        kernel,
-        out_shape=(
+        total = jnp.transpose(total)[:8]
+        total_ref[...] = total
+        if tail:
+            write_split(o_refs[0], half, total[0:1])
+        project_into(o_refs, scaled_ref, w_ref, table_ref[slot] * width, width)
+
+    return pl.pallas_call(
+        kernel,
+        out_shape=[
             jax.ShapeDtypeStruct((chunk, slab), jnp.bfloat16),
             jax.ShapeDtypeStruct((8, chunk), jnp.float32),
-            jax.ShapeDtypeStruct((chunk, width), jnp.bfloat16),
-        ),
+        ]
+        + [jax.ShapeDtypeStruct((half + (tail if h == 0 else 0), width), jnp.bfloat16) for h in range(halves)],
         in_specs=[SCALARS] + [WHOLE] * (2 + count),
-        out_specs=(WHOLE, WHOLE, WHOLE),
+        out_specs=[WHOLE] * (2 + halves),
         compiler_params=LIMIT,
         cost_estimate=effort(2 * chunk * slab * width),
     )(table, gain, weight, *pieces)
@@ -122,30 +148,40 @@
 
 def attend(projected, received, totals, bias, cosine, sine, mask, earlier, heads, used, features):
     chunk = projected.shape[0]
+    halves = len(received)
+    half = chunk // halves
+    counts = [len(parts) for parts in received]
     group = heads // used
     own_cols = heads * HD
     used_cols = used * HD
-    parts = len(received)
+    parts = sum(counts)
+    summed = len(totals)
     past = len(earlier)
     scale = HD ** (-0.5)
 
     def kernel(p_ref, bias_ref, cos_ref, sin_ref, mask_ref, *refs):
-        part_refs = refs[:parts]
-        total_refs = refs[parts : 2 * parts + 1]
-        past_refs = refs[2 * parts + 1 : 2 * parts + 1 + 2 * past]
-        o_ref, k_ref, v_ref = refs[2 * parts + 1 + 2 * past :]
+        part_refs = [refs[sum(counts[:h]) : sum(counts[: h + 1])] for h in range(halves)]
+        total_refs = refs[parts : parts + summed]
+        past_refs = refs[parts + summed : parts + summed + 2 * past]
+        *o_refs, k_ref, v_ref = refs[parts + summed + 2 * past :]
         total = total_refs[0][0:1, :]
         for ref in total_refs[1:]:
             total = total + ref[0:1, :]
+        for ref in [r for parts_of in part_refs for r in parts_of if r.shape[0] > half]:
+            total = total + read_split(ref, half, chunk)
         inverse = lax.rsqrt(total / features + EPSILON)
         inverse = jnp.transpose(jnp.broadcast_to(inverse, (HD, chunk)))
         cosine_rows = cos_ref[...]
         sine_rows = sin_ref[...]
 
         def columns(start):
-            value = p_ref[:, start : start + HD]
-            for ref in part_refs:
-                value = value + ref[:, start : start + HD].astype(jnp.float32)
+            pieces = []
+            for h in range(halves):
+                piece = p_ref[h * half : (h + 1) * half, start : start + HD]
+                for ref in part_refs[h]:
+                    piece = piece + ref[:half, start : start + HD].astype(jnp.float32)
+                pieces.append(piece)
+            value = jnp.concatenate(pieces, axis=0) if halves > 1 else pieces[0]
             return value * inverse + bias_ref[:, start : start + HD]
 
         def rotate(value):
@@ -170,25 +206,26 @@
                 weights = jnp.where(allowed, jnp.exp(scores - jnp.max(scores, axis=1, keepdims=True)), 0.0)
                 denominator = jnp.sum(weights, axis=1, keepdims=True)
                 mixed = jnp.dot(weights.astype(jnp.bfloat16), values, preferred_element_type=jnp.float32)
-                o_ref[:, start : start + HD] = (mixed / denominator).astype(jnp.bfloat16)
-
-    return pl.pallas_call(
-        kernel,
-        out_shape=(
-            jax.ShapeDtypeStruct((chunk, own_cols), jnp.bfloat16),
-            jax.ShapeDtypeStruct((chunk, used_cols), jnp.bfloat16),
-            jax.ShapeDtypeStruct((chunk, used_cols), jnp.bfloat16),
-        ),
-        in_specs=[WHOLE] * (5 + 2 * parts + 1 + 2 * past),
-        out_specs=(WHOLE, WHOLE, WHOLE),
+                attended = (mixed / denominator).astype(jnp.bfloat16)
+                for h, o_ref in enumerate(o_refs):
+                    o_ref[:, start : start + HD] = attended[h * half : (h + 1) * half]
+
+    return pl.pallas_call(
+        kernel,
+        out_shape=[jax.ShapeDtypeStruct((half, own_cols), jnp.bfloat16)] * halves
+        + [jax.ShapeDtypeStruct((chunk, used_cols), jnp.bfloat16)] * 2,
+        in_specs=[WHOLE] * (5 + parts + summed + 2 * past),
+        out_specs=[WHOLE] * (halves + 2),
         compiler_params=LIMIT,
         cost_estimate=effort(1 << 29),
-    )(projected, bias, cosine, sine, mask, *received, *totals, *[a for pair in earlier for a in pair])
+    )(projected, bias, cosine, sine, mask, *[p for parts in received for p in parts], *totals, *[a for pair in earlier for a in pair])
 
 
 def mix_blocks(table, slots, blocks, weight, held, so_far, cores):
     count = len(blocks)
-    chunk, depth = blocks[0].shape
+    pieces = len(blocks[0])
+    depth = blocks[0][0].shape[1]
+    chunk = blocks[0][0].shape[0] * pieces
     slab = weight.shape[2]
     share = chunk // cores
     tile = min(slab, 512)
@@ -196,10 +233,11 @@
     steps = [(i, b) for i in range(slab // tile) for b in range(count) if b not in near]
     buffers = min(4, len(steps))
     ready = [held[slots[b]] for b in near]
-    inputs = [*blocks, *ready] + ([] if so_far is None else [so_far])
+    inputs = [*ready, *[p for block in blocks for p in block]] + ([] if so_far is None else [so_far])
 
     def kernel(table_ref, w_ref, *refs):
         outs = refs[len(inputs) : len(inputs) + cores]
+        rows_of = [refs[len(ready) + b * pieces : len(ready) + (b + 1) * pieces] for b in range(count)]
         fetches = []
         for step, (i, b) in enumerate(steps):
             row = pl.multiple_of(table_ref[slots[b]] * depth, 128)
@@ -213,17 +251,18 @@
             )
         for fetch in fetches[:buffers]:
             fetch.start()
+        left = [jnp.concatenate([r[...] for r in p], axis=0) if pieces > 1 else p[0][...] for p in rows_of]
         for i in range(slab // tile):
             spot = slice(i * tile, (i + 1) * tile)
             out = None if so_far is None else refs[len(inputs) - 1][:, spot]
             for b in near + [b for b in range(count) if b not in near]:
                 if b in near:
-                    rows = refs[count + near.index(b)][:, spot]
+                    rows = refs[near.index(b)][:, spot]
                 else:
                     step = steps.index((i, b))
                     fetches[step].wait()
                     rows = refs[-2][step % buffers]
-                term = jnp.dot(refs[b][...], rows, preferred_element_type=jnp.float32)
+                term = jnp.dot(left[b], rows, preferred_element_type=jnp.float32)
                 out = term if out is None else out + term
                 if b not in near and step + buffers < len(steps):
                     fetches[step + buffers].start()
@@ -242,6 +281,60 @@
         compiler_params=pltpu.CompilerParams(vmem_limit_bytes=8 << 20),
         cost_estimate=effort(2 * count * chunk * depth * slab),
     )(table, weight, *inputs)
+
+
+def fold(part_x, part_y, from_x, from_y, total):
+    half, _ = part_x.shape
+    chunk = total.shape[1]
+
+    def kernel(x_ref, y_ref, from_x_ref, from_y_ref, total_ref, to_y_ref, to_x_ref, pair_ref):
+        to_y_ref[:half] = (y_ref[...].astype(jnp.float32) + from_x_ref[:half].astype(jnp.float32)).astype(jnp.bfloat16)
+        to_x_ref[...] = (x_ref[...].astype(jnp.float32) + from_y_ref[...].astype(jnp.float32)).astype(jnp.bfloat16)
+        pair = total_ref[0:1, :] + read_split(from_x_ref, half, chunk)
+        write_split(to_y_ref, half, pair)
+        pair_ref[...] = jnp.broadcast_to(pair, (8, chunk))
+
+    return pl.pallas_call(
+        kernel,
+        out_shape=[
+            jax.ShapeDtypeStruct(from_x.shape, jnp.bfloat16),
+            jax.ShapeDtypeStruct(from_y.shape, jnp.bfloat16),
+            jax.ShapeDtypeStruct(total.shape, jnp.float32),
+        ],
+        in_specs=[WHOLE] * 5,
+        out_specs=[WHOLE] * 3,
+        compiler_params=LIMIT,
+        cost_estimate=effort(1 << 26),
+    )(part_x, part_y, from_x, from_y, total)
+
+
+def pick(table, slots, choices, joined=False):
+    shape = choices[0].shape
+    count = len(slots)
+
+    def kernel(table_ref, *refs):
+        for i, slot in enumerate(slots):
+            for k in range(len(choices)):
+
+                @pl.when(table_ref[slot] == k)
+                def _():
+                    if joined:
+                        refs[-1][i * shape[0] : (i + 1) * shape[0]] = refs[k][...]
+                    else:
+                        refs[len(choices) + i][...] = refs[k][...]
+
+    if joined:
+        outs = [jax.ShapeDtypeStruct((count * shape[0], shape[1]), choices[0].dtype)]
+    else:
+        outs = [jax.ShapeDtypeStruct(shape, choices[0].dtype)] * count
+    return pl.pallas_call(
+        kernel,
+        out_shape=outs,
+        in_specs=[SCALARS] + [WHOLE] * len(choices),
+        out_specs=[WHOLE] * len(outs),
+        compiler_params=LIMIT,
+        cost_estimate=effort(1 << 24),
+    )(table, *choices)
 
 
 def leave(rows, own_sum, pieces):
@@ -335,21 +428,16 @@
                 for k in range(CHUNKS)
             ]
 
-        def collect(slabs):
+        def collect(found):
+            sent = pick(table, range(picks, picks + CHUNKS), found)
             pieces = []
             for j in range(CHUNKS):
                 pairs = [
                     (c * size_gz + d, (d + j) % size_gy * size_gz + c) for c in range(size_gy) for d in range(size_gz)
                 ]
-                piece = sum_of([(flag(sections + j * CHUNKS + k), slabs[k]) for k in range(CHUNKS)])
-                pieces.append(lax.ppermute(piece, ("gy", "gz"), pairs))
-            return jnp.concatenate(
-                [
-                    sum_of([(flag(sections + CHUNKS * CHUNKS + d * CHUNKS + j), pieces[j]) for j in range(CHUNKS)])
-                    for d in range(size_gz)
-                ],
-                axis=0,
-            )
+                pieces.append(lax.ppermute(sent[j], ("gy", "gz"), pairs))
+            (rows,) = pick(table, range(picks + CHUNKS, picks + CHUNKS + size_gz), pieces, joined=True)
+            return rows
     else:
 
         def spread(block):
@@ -359,7 +447,8 @@
             pieces = lax.dynamic_index_in_dim(pieces, index_gz, 1, keepdims=False)
             return [pieces[k] for k in range(CHUNKS)]
 
-        def collect(slabs):
+        def collect(found):
+            slabs = [pick(table, [mine + 1], found[k : k + sections])[0] for k in range(CHUNKS)]
             rows = gathered(jnp.stack(slabs), "gz", 1).reshape(tokens, slab)
             wide = lax.all_to_all(rows, "gy", split_axis=0, concat_axis=1, tiled=True)
             piece = wide.shape[1] // size_gz
@@ -370,8 +459,6 @@
         for condition, value in choices[1:]:
             chosen = jnp.where(condition, value, chosen)
         return chosen
-
-    entering = [piece for m in range(micro_count) for piece in spread(micro_inputs[m])]
 
     gain_slab = lax.dynamic_slice_in_dim(norm_gain[0], index_gy * slab, slab, 0)[None, :]
     own_bias = jnp.concatenate(
@@ -402,16 +489,23 @@
         ).astype(jnp.float32)
         for t in range(ticks)
     ]
-    conditions = [index_section == s for s in range(sections)]
-    if even:
-        conditions += [lax.rem(index_gz + j, size_gy) == k for j in range(CHUNKS) for k in range(CHUNKS)]
-        conditions += [lax.rem(index_gy + size_gy - j, size_gz) == d for d in range(size_gz) for j in range(CHUNKS)]
-    flags = jnp.broadcast_to(jnp.stack(conditions).astype(jnp.float32)[:, None], (len(conditions), 128))
     far_first = offsets[::-1]
+    square = size_gx == size_gy == 2
     targets = [chip_at(dx, dy) for dx, dy in far_first]
     sources = [chip_at(size_gx - dx if dx else 0, size_gy - dy if dy else 0) for dx, dy in offsets]
-    table = jnp.stack(targets + sources + [me]).astype(jnp.int32)
     mine = 2 * len(offsets)
+    choice = [index_section, jnp.minimum(index_section, 1)]
+    picks = mine + 1 + len(choice)
+    if even:
+        choice += [lax.rem(index_gz + j, size_gy) + index_section for j in range(CHUNKS)]
+        choice += [lax.rem(index_gy + size_gy - d, size_gz) for d in range(size_gz)]
+    table = jnp.stack(targets + sources + [me] + choice).astype(jnp.int32)
+    early = [gain_slab, own_bias, *cosines, *sines, *masks]
+    (table, early, micro_inputs) = lax.optimization_barrier((table, early, micro_inputs))
+    gain_slab, own_bias = early[:2]
+    cosines, sines, masks = (early[2 + i * ticks : 2 + (i + 1) * ticks] for i in range(3))
+    entering = [piece for m in range(micro_count) for piece in spread(micro_inputs[m])]
+
     copies = []
     everything = slice(None)
     for chip in range(group):
@@ -430,28 +524,38 @@
             return 0, pl.ds(pl.multiple_of(table_ref[slot] * own_cols, 128), own_cols)
 
         held_copies.append((0, where, i, (everything,)))
-    early = [gain_slab, own_bias, *cosines, *sines, *masks]
-    table, flags, weights = resident([table, flags], early, [q_weight, kv_weight], copies, [(slab, group * width)])
+    table, weights = resident([table], early, [q_weight, kv_weight], copies, [(slab, group * width)])
     _, *held = resident([table], [], [out_weight], held_copies, [(own_cols, slab)] * kept)
     held = {mine - 1 - i: w for i, w in enumerate(held)}
     mixing_weight = pltpu.with_memory_space_constraint(out_weight, pltpu.HBM)
 
-    def flag(i):
-        return flags[i : i + 1, :1] > 0.5
-
     def layer(own_rows, tick, earlier):
         pieces = [own_rows] + [around(own_rows, "gz", -j) for j in range(1, size_gz)]
-        scaled, total, part = enter(table, 0, pieces, gain_slab, weights, width)
-        received = []
-        for k, o in enumerate(far_first):
-            if k:
-                part = project_block(table, k, scaled, weights, width, jnp.bfloat16)
-            received.append(to_offset(part, *o))
-        totals = [total]
-        for o in far_first:
-            totals.append(to_offset(total, *o))
-        projected = project_block(table, mine, scaled, weights, width, jnp.float32)
-        attended, keys, values = attend(
+        scaled, total, *part = enter(table, 0, pieces, gain_slab, weights, width, 2 if square else 1)
+        if square:
+            from_x = to_offset(part[0], 1, 0)
+            from_y = to_offset(part[1], 0, 1)
+            later_y, near_y = project_block(table, 2, scaled, weights, width, jnp.bfloat16, 2)
+            direct_y = to_offset(near_y, 0, 1)
+            near_x, later_x = project_block(table, 1, scaled, weights, width, jnp.bfloat16, 2)
+            direct_x = to_offset(near_x, 1, 0)
+            to_y, to_x, total = fold(later_x, later_y, from_x, from_y, total)
+            folded_y = to_offset(to_y, 0, 1)
+            folded_x = to_offset(to_x, 1, 0)
+            received = [[direct_x, folded_y], [direct_y, folded_x]]
+            totals = [total]
+        else:
+            received = [[]]
+            totals = [total]
+            part = part[0]
+            for k, o in enumerate(far_first):
+                if k:
+                    (part,) = project_block(table, k, scaled, weights, width, jnp.bfloat16)
+                received[0].append(to_offset(part, *o))
+            for o in far_first:
+                totals.append(to_offset(total, *o))
+        (projected,) = project_block(table, mine, scaled, weights, width, jnp.float32)
+        *attended, keys, values = attend(
             projected,
             received,
             totals,
@@ -466,9 +570,18 @@
         )
         seen = [(keys, values)] + earlier
         arrived = []
-        for o in offsets:
-            arrived.append(to_offset(attended, *o))
-        (sums,) = mix_blocks(table, [mine], [attended], mixing_weight, held, None, 1)
+        if square:
+            x_upper = to_offset(attended[0], 1, 0)
+            y_lower = to_offset(attended[1], 0, 1)
+            x_lower = to_offset(attended[1], 1, 0)
+            y_upper = to_offset(attended[0], 0, 1)
+            far_upper = to_offset(x_upper, 0, 1)
+            far_lower = to_offset(y_lower, 1, 0)
+            arrived = [(y_upper, y_lower), (x_upper, x_lower), (far_upper, far_lower)]
+        else:
+            for o in offsets:
+                arrived.append((to_offset(attended[0], *o),))
+        (sums,) = mix_blocks(table, [mine], [tuple(attended)], mixing_weight, held, None, 1)
         back = list(range(len(offsets), mine))
         if len(offsets) > 1:
             (sums,) = mix_blocks(table, back[:-1], arrived[:-1], mixing_weight, held, sums, 1)
@@ -483,7 +596,7 @@
         if carried is None:
             current = entering[0]
         elif tick < jobs:
-            current = jnp.where(flag(0), entering[tick], carried)
+            (current,) = pick(table, [mine + 2], [entering[tick], carried])
         else:
             current = carried
         result, earlier = layer(current, tick, earlier)
@@ -491,8 +604,8 @@
         if tick < ticks - 1:
             carried = lax.ppermute(result, "section", [(i, i + 1) for i in range(sections - 1)])
 
-    stored = [sum_of([(flag(s), results[job + s]) for s in range(sections)]) for job in range(jobs)]
-    return jnp.stack([collect(stored[m * CHUNKS : (m + 1) * CHUNKS]) for m in range(micro_count)])[None]
+    cuts = [results[m * CHUNKS : (m + 1) * CHUNKS + sections - 1] for m in range(micro_count)]
+    return jnp.stack([collect(found) for found in cuts])[None]
 
 
 def solution(mesh):

time: 307 us -> 264 us (0.86)
  waiting for transfers between devices: 139 us -> 87.4 us
  starting transfers between devices: 69.6 us -> 85 us
  between operations: 8.44 us -> 3.43 us
    ppermute x45 -> x60, waiting for transfers between devices: 102 us -> 40 us  [to_offset(): return lax.ppermute(value, ('gx', 'gy'), pairs)]
    ppermute x45 -> x60, starting transfers between devices: 46.1 us -> 59.8 us  [to_offset(): return lax.ppermute(value, ('gx', 'gy'), pairs)]
    ppermute x2, waiting for transfers between devices: 0.09 us -> 6.18 us  [spread(): pieces.append(lax.ppermute(piece, ('gy', 'gz'), pairs))]
    ppermute x2, starting transfers between devices: 5.04 us -> 1.17 us  [spread(): pieces.append(lax.ppermute(piece, ('gy', 'gz'), pairs))]
    pallas_call x25 -> x33, Pallas kernels: 43 us -> 44.7 us  [the longest x15 25.4 us: project_block(): pl.pallas_call(kernel, out_shape=[jax.ShapeDtypeStruct((rows.shape[0] //...]
  transfers between devices with their start and end apart: 63 -> 78, of which waited for: 33 -> 43; matrix products, arithmetic and copies ran while one was open for 2% -> 0% of each run, Pallas kernels for 13% -> 22%
where the time goes in v1:
time: 264 us; the launch traced here: 262 us
  waiting for transfers between devices  87.4 us (33%)
  starting transfers between devices  85 us (32%)
  Pallas kernels  80.2 us (30%)
  local copies, waits for them, and re-layouts  4.1 us (2%)
  between operations  3.43 us (1%)
    ppermute x60, starting transfers between devices, to_offset(): return lax.ppermute(value, ('gx', 'gy'), pairs)  59.8 us
    ppermute x60, waiting for transfers between devices, to_offset(): return lax.ppermute(value, ('gx', 'gy'), pairs)  40 us
    pallas_call x15, Pallas kernels, project_block(): pl.pallas_call(kernel, out_shape=[jax.ShapeDtypeStruct((rows.shape[0] //...  25.4 us
    pallas_call x15, Pallas kernels, mix_blocks(): pl.pallas_call(kernel, out_shape=[jax.ShapeDtypeStruct((share, slab), jnp...  22.7 us
    ppermute x4, waiting for transfers between devices, body(): lax.ppermute(result, 'section', [(i, i + 1) for i in range(sections - 1)])  22.4 us
    ppermute x4, starting transfers between devices, body(): lax.ppermute(result, 'section', [(i, i + 1) for i in range(sections - 1)])  16.9 us
    ppermute x10, waiting for transfers between devices, around(): lax.ppermute(value, axis, [(i, (i + steps) % count) for i in range(count)])  13.7 us
    pallas_call x2, Pallas kernels, resident(): pl.pallas_call(kernel, out_shape=[(pltpu.SMEM if v.dtype == jnp.int32 els...  12.5 us
  transfers between devices with their start and end apart: 78, of which 43 were waited for; matrix products, arithmetic and copies ran while one was open for 0% of the time, Pallas kernels for 22%

profile of v1, /device:TPU:0, one launch (start us, length us, event | category | flops | bytes accessed | tf_op | source)
XLA Modules:
  0.0 262.0 jit_solution(15068336170673259054)
XLA Ops:
  9.2 6.2 %collective-permute-done = bf16[64,2048]{1,0:T(8,128)(2,1)S(1)} collective-permute-done((bf16[64,2048]{1,0:T(8,128)(2,1)S(1)}, bf16[64,2048]{1,0:T(8,128)(2,1)S(1)}, u32[]{:S(2)}, u32[]{:S(2)}) %collective-permute-start) | collective-permute-done | bytes 262176 | tf_op jit(solution)/shard_map/ppermute | solution.py:425
  15.4 2.9 %collective-permute-start.2 = (bf16[64,2048]{1,0:T(8,128)(2,1)S(1)}, bf16[64,2048]{1,0:T(8,128)(2,1)S(1)}, u32[]{:S(2)}, u32[]{:S(2)}) collective-permute-start(bf16[64,2048]{1,0:T(8,128)(2,1)S(1)} %get-tuple-element.229.refs_0_.x_ref), channel_id=1, source_target_pairs={{0,1},{1,0},{2,3},{3,2},{4,5},{5,4},{6,7},{7,6},{8,9},{9,8},{10,11... | collective-permute-start | bytes 786440 | tf_op jit(solution)/shard_map/ppermute | solution.py:359
  18.3 7.8 %shard_map.73 = (s32[13]{0:T(128)S(4)}, bf16[2048,5120]{1,0:T(8,128)(2,1)S(1)}) custom-call(s32[13]{0:T(128)S(1)} %stack.46.refs_0_, bf16[1,2048,4096]{2,1,0:T(8,128)(2,1)} %refs_1_.2, bf16[1,2,2048,512]{3,2,1,0:T(8,128)(2,1)} %refs_2_.1, f32[1,2048]{1,0:T(1,128)S(1)} %constant_dynamic-slice_fusion.3.refs_3_.gain_ref, ...), custom_call_target="tpu_custom_call" | custom-call | flops 4294967296 | tf_op jit(solution)/shard_map/pallas_call | solution.py:53
  26.1 2.1 shard_map.75
  28.2 1.8 collective-permute-start.4
  30.7 1.7 shard_map.78
  32.4 1.7 shard_map.77
  34.1 1.7 collective-permute-done.5.from_y_ref
  41.7 3.2 %collective-permute-done.7.refs_2_ = bf16[64,1280]{1,0:T(8,128)(2,1)S(1)} collective-permute-done((bf16[64,1280]{1,0:T(8,128)(2,1)S(1)}, bf16[64,1280]{1,0:T(8,128)(2,1)S(1)}, u32[]{:S(2)}, u32[]{:S(2)}) %collective-permute-start.7) | collective-permute-done | bytes 163872 | tf_op jit(solution)/shard_map/ppermute | solution.py:408
  46.0 2.3 shard_map.80
  48.3 1.7 collective-permute-start.11
  52.4 4.7 %shard_map.74 = (s32[13]{0:T(128)S(4)}, bf16[1024,2048]{1,0:T(8,128)(2,1)S(1)}, bf16[1024,2048]{1,0:T(8,128)(2,1)S(1)}, bf16[1024,2048]{1,0:T(8,128)(2,1)S(1)}) custom-call(s32[13]{0:T(128)S(4)} %get-tuple-element.132.refs_0_.table_ref, bf16[1,4096,2048]{2,1,0:T(8,128)(2,1)} %w_ref.29), custom_call_target="tpu_custom_call" | custom-call | flops 4294967296 | tf_op jit(solution)/shard_map/pallas_call | solution.py:53
  57.1 1.7 collective-permute-start.10
  59.8 2.5 shard_map.81.refs_6_
  66.2 3.5 %collective-permute-start.16 = (bf16[64,2048]{1,0:T(8,128)(2,1)S(1)}, bf16[64,2048]{1,0:T(8,128)(2,1)S(1)}, u32[]{:S(2)}, u32[]{:S(2)}) collective-permute-start(bf16[64,2048]{1,0:T(8,128)(2,1)S(1)} %shard_map.84.refs_0_), channel_id=1, source_target_pairs={{0,8},{8,16},{16,24},{1,9},{9,17},{17,25},{2,10},{10,18},{18,26},{... | collective-permute-start | bytes 786440 | tf_op jit(solution)/shard_map/ppermute | solution.py:605
  70.4 5.1 %collective-permute-done.16.refs_1_ = bf16[64,2048]{1,0:T(8,128)(2,1)S(1)} collective-permute-done((bf16[64,2048]{1,0:T(8,128)(2,1)S(1)}, bf16[64,2048]{1,0:T(8,128)(2,1)S(1)}, u32[]{:S(2)}, u32[]{:S(2)}) %collective-permute-start.16) | collective-permute-done | bytes 262176 | tf_op jit(solution)/shard_map/ppermute | solution.py:605
  77.4 2.1 shard_map.86
  80.9 1.7 shard_map.89
  82.6 1.7 shard_map.88
  84.3 2.2 collective-permute-done.20.from_y_ref
  92.3 3.3 %collective-permute-done.22.refs_2_ = bf16[64,1280]{1,0:T(8,128)(2,1)S(1)} collective-permute-done((bf16[64,1280]{1,0:T(8,128)(2,1)S(1)}, bf16[64,1280]{1,0:T(8,128)(2,1)S(1)}, u32[]{:S(2)}, u32[]{:S(2)}) %collective-permute-start.22) | collective-permute-done | bytes 163872 | tf_op jit(solution)/shard_map/ppermute | solution.py:408
  105.8 2.5 shard_map.92.refs_6_
  112.2 4.4 %collective-permute-start.31 = (bf16[64,2048]{1,0:T(8,128)(2,1)S(1)}, bf16[64,2048]{1,0:T(8,128)(2,1)S(1)}, u32[]{:S(2)}, u32[]{:S(2)}) collective-permute-start(bf16[64,2048]{1,0:T(8,128)(2,1)S(1)} %shard_map.95.refs_1_), channel_id=1, source_target_pairs={{0,8},{8,16},{16,24},{1,9},{9,17},{17,25},{2,10},{10,18},{18,26},{... | collective-permute-start | bytes 786440 | tf_op jit(solution)/shard_map/ppermute | solution.py:605
  116.5 5.8 %collective-permute-done.31.refs_0_.x_ref = bf16[64,2048]{1,0:T(8,128)(2,1)S(1)} collective-permute-done((bf16[64,2048]{1,0:T(8,128)(2,1)S(1)}, bf16[64,2048]{1,0:T(8,128)(2,1)S(1)}, u32[]{:S(2)}, u32[]{:S(2)}) %collective-permute-start.31) | collective-permute-done | bytes 262176 | tf_op jit(solution)/shard_map/ppermute | solution.py:605
  123.9 2.1 shard_map.96
  127.9 1.7 shard_map.99
  129.6 1.7 shard_map.98
  131.3 1.7 collective-permute-done.35.from_y_ref
  138.9 3.3 %collective-permute-done.37.refs_2_ = bf16[64,1280]{1,0:T(8,128)(2,1)S(1)} collective-permute-done((bf16[64,1280]{1,0:T(8,128)(2,1)S(1)}, bf16[64,1280]{1,0:T(8,128)(2,1)S(1)}, u32[]{:S(2)}, u32[]{:S(2)}) %collective-permute-start.37) | collective-permute-done | bytes 163872 | tf_op jit(solution)/shard_map/ppermute | solution.py:408
  152.3 2.5 shard_map.102.refs_6_
  158.7 4.6 %collective-permute-start.46 = (bf16[64,2048]{1,0:T(8,128)(2,1)S(1)}, bf16[64,2048]{1,0:T(8,128)(2,1)S(1)}, u32[]{:S(2)}, u32[]{:S(2)}) collective-permute-start(bf16[64,2048]{1,0:T(8,128)(2,1)S(1)} %shard_map.105.refs_2_), channel_id=1, source_target_pairs={{0,8},{8,16},{16,24},{1,9},{9,17},{17,25},{2,10},{10,18},{18,26},{... | collective-permute-start | bytes 786440 | tf_op jit(solution)/shard_map/ppermute | solution.py:605
  163.3 5.6 %collective-permute-done.46.refs_0_.x_ref = bf16[64,2048]{1,0:T(8,128)(2,1)S(1)} collective-permute-done((bf16[64,2048]{1,0:T(8,128)(2,1)S(1)}, bf16[64,2048]{1,0:T(8,128)(2,1)S(1)}, u32[]{:S(2)}, u32[]{:S(2)}) %collective-permute-start.46) | collective-permute-done | bytes 262176 | tf_op jit(solution)/shard_map/ppermute | solution.py:605
  170.5 2.1 shard_map.106
  174.5 1.7 shard_map.109
  176.2 1.7 shard_map.108
  183.7 1.7 shard_map.107.p_ref
  185.4 3.3 %collective-permute-done.52.refs_2_ = bf16[64,1280]{1,0:T(8,128)(2,1)S(1)} collective-permute-done((bf16[64,1280]{1,0:T(8,128)(2,1)S(1)}, bf16[64,1280]{1,0:T(8,128)(2,1)S(1)}, u32[]{:S(2)}, u32[]{:S(2)}) %collective-permute-start.52) | collective-permute-done | bytes 163872 | tf_op jit(solution)/shard_map/ppermute | solution.py:408
  198.9 2.5 shard_map.112.refs_6_
  205.3 4.4 %collective-permute-start.61 = (bf16[64,2048]{1,0:T(8,128)(2,1)S(1)}, bf16[64,2048]{1,0:T(8,128)(2,1)S(1)}, u32[]{:S(2)}, u32[]{:S(2)}) collective-permute-start(bf16[64,2048]{1,0:T(8,128)(2,1)S(1)} %shard_map.115.refs_3_), channel_id=1, source_target_pairs={{0,8},{8,16},{16,24},{1,9},{9,17},{17,25},{2,10},{10,18},{18,26},{... | collective-permute-start | bytes 786440 | tf_op jit(solution)/shard_map/ppermute | solution.py:605
  209.6 5.8 %collective-permute-done.61.refs_0_.x_ref = bf16[64,2048]{1,0:T(8,128)(2,1)S(1)} collective-permute-done((bf16[64,2048]{1,0:T(8,128)(2,1)S(1)}, bf16[64,2048]{1,0:T(8,128)(2,1)S(1)}, u32[]{:S(2)}, u32[]{:S(2)}) %collective-permute-start.61) | collective-permute-done | bytes 262176 | tf_op jit(solution)/shard_map/ppermute | solution.py:605
  217.0 2.1 shard_map.116
  221.0 1.7 shard_map.119
  222.7 1.7 shard_map.118
  224.4 1.7 collective-permute-done.65.from_y_ref
  232.0 3.3 %collective-permute-done.67.refs_2_ = bf16[64,1280]{1,0:T(8,128)(2,1)S(1)} collective-permute-done((bf16[64,1280]{1,0:T(8,128)(2,1)S(1)}, bf16[64,1280]{1,0:T(8,128)(2,1)S(1)}, u32[]{:S(2)}, u32[]{:S(2)}) %collective-permute-start.67) | collective-permute-done | bytes 163872 | tf_op jit(solution)/shard_map/ppermute | solution.py:408
  245.8 2.5 shard_map.122.refs_6_
  253.0 3.0 %collective-permute-start.77 = (bf16[64,2048]{1,0:T(8,128)(2,1)S(1)}, bf16[64,2048]{1,0:T(8,128)(2,1)S(1)}, u32[]{:S(2)}, u32[]{:S(2)}) collective-permute-start(bf16[64,2048]{1,0:T(8,128)(2,1)S(1)} %get-tuple-element.222), channel_id=1, source_target_pairs={{0,2},{1,0},{2,3},{3,1},{4,6},{5,4},{6,7},{7,5},{8,10},{9,8},{10,1... | collective-permute-start | bytes 786440 | tf_op jit(solution)/shard_map/ppermute | solution.py:438
  256.0 5.2 %collective-permute-done.77.refs_1_ = bf16[64,2048]{1,0:T(8,128)(2,1)S(1)} collective-permute-done((bf16[64,2048]{1,0:T(8,128)(2,1)S(1)}, bf16[64,2048]{1,0:T(8,128)(2,1)S(1)}, u32[]{:S(2)}, u32[]{:S(2)}) %collective-permute-start.77) | collective-permute-done | bytes 262176 | tf_op jit(solution)/shard_map/ppermute | solution.py:438
  (192 shorter events, 116.5 us)
Async XLA Ops:
  8.0 7.4 %collective-permute-start = (bf16[64,2048]{1,0:T(8,128)(2,1)S(1)}, bf16[64,2048]{1,0:T(8,128)(2,1)S(1)}, u32[]{:S(2)}, u32[]{:S(2)}) collective-permute-start(bf16[64,2048]{1,0:T(8,128)(2,1)S(1)} %get-tuple-element.231), channel_id=1, source_target_pairs={{0,1},{1,3},{2,0},{3,2},{4,5},{5,7},{6,4},{7,6},{8,9},{9,11},{10,8... | collective-permute-start | bytes 786440 | tf_op jit(solution)/shard_map/ppermute | solution.py:425
  8.5 6.9 %collective-permute-start.1 = (bf16[64,2048]{1,0:T(8,128)(2,1)S(1)}, bf16[64,2048]{1,0:T(8,128)(2,1)S(1)}, u32[]{:S(2)}, u32[]{:S(2)}) collective-permute-start(bf16[64,2048]{1,0:T(8,128)(2,1)S(1)} %get-tuple-element.230), channel_id=1, source_target_pairs={{0,0},{1,2},{2,1},{3,3},{4,4},{5,6},{6,5},{7,7},{8,8},{9,10},{10,9... | collective-permute-start | bytes 786440 | tf_op jit(solution)/shard_map/ppermute | solution.py:425
  15.4 10.7 %collective-permute-start.2 = (bf16[64,2048]{1,0:T(8,128)(2,1)S(1)}, bf16[64,2048]{1,0:T(8,128)(2,1)S(1)}, u32[]{:S(2)}, u32[]{:S(2)}) collective-permute-start(bf16[64,2048]{1,0:T(8,128)(2,1)S(1)} %get-tuple-element.229.refs_0_.x_ref), channel_id=1, source_target_pairs={{0,1},{1,0},{2,3},{3,2},{4,5},{5,4},{6,7},{7,6},{8,9},{9,8},{10,11... | collective-permute-start | bytes 786440 | tf_op jit(solution)/shard_map/ppermute | solution.py:359
  28.2 7.6 %collective-permute-start.4 = (bf16[72,1280]{1,0:T(8,128)(2,1)S(1)}, bf16[72,1280]{1,0:T(8,128)(2,1)S(1)}, u32[]{:S(2)}, u32[]{:S(2)}) collective-permute-start(bf16[72,1280]{1,0:T(8,128)(2,1)S(1)} %get-tuple-element.140), channel_id=1, source_target_pairs={{0,4},{2,6},{4,0},{6,2},{1,5},{3,7},{5,1},{7,3},{8,12},{10,14},{12... | collective-permute-start | bytes 552968 | tf_op jit(solution)/shard_map/ppermute | solution.py:408
  35.9 10.0 %collective-permute-start.6 = (bf16[72,1280]{1,0:T(8,128)(2,1)S(1)}, bf16[72,1280]{1,0:T(8,128)(2,1)S(1)}, u32[]{:S(2)}, u32[]{:S(2)}) collective-permute-start(bf16[72,1280]{1,0:T(8,128)(2,1)S(1)} %get-tuple-element.143), channel_id=1, source_target_pairs={{0,2},{2,0},{4,6},{6,4},{1,3},{3,1},{5,7},{7,5},{8,10},{10,8},{12,... | collective-permute-start | bytes 552968 | tf_op jit(solution)/shard_map/ppermute | solution.py:408
  37.2 7.7 %collective-permute-start.7 = (bf16[64,1280]{1,0:T(8,128)(2,1)S(1)}, bf16[64,1280]{1,0:T(8,128)(2,1)S(1)}, u32[]{:S(2)}, u32[]{:S(2)}) collective-permute-start(bf16[64,1280]{1,0:T(8,128)(2,1)S(1)} %get-tuple-element.144), channel_id=1, source_target_pairs={{0,2},{2,0},{4,6},{6,4},{1,3},{3,1},{5,7},{7,5},{8,10},{10,8},{12,... | collective-permute-start | bytes 491528 | tf_op jit(solution)/shard_map/ppermute | solution.py:408
  38.0 6.9 %collective-permute-start.3 = (bf16[64,1280]{1,0:T(8,128)(2,1)S(1)}, bf16[64,1280]{1,0:T(8,128)(2,1)S(1)}, u32[]{:S(2)}, u32[]{:S(2)}) collective-permute-start(bf16[64,1280]{1,0:T(8,128)(2,1)S(1)} %get-tuple-element.137), channel_id=1, source_target_pairs={{0,4},{2,6},{4,0},{6,2},{1,5},{3,7},{5,1},{7,3},{8,12},{10,14},{12... | collective-permute-start | bytes 491528 | tf_op jit(solution)/shard_map/ppermute | solution.py:408
  38.8 7.2 %collective-permute-start.8 = (bf16[64,1280]{1,0:T(8,128)(2,1)S(1)}, bf16[64,1280]{1,0:T(8,128)(2,1)S(1)}, u32[]{:S(2)}, u32[]{:S(2)}) collective-permute-start(bf16[64,1280]{1,0:T(8,128)(2,1)S(1)} %get-tuple-element.145), channel_id=1, source_target_pairs={{0,4},{2,6},{4,0},{6,2},{1,5},{3,7},{5,1},{7,3},{8,12},{10,14},{12... | collective-permute-start | bytes 491528 | tf_op jit(solution)/shard_map/ppermute | solution.py:408
  48.3 10.6 %collective-permute-start.11 = (bf16[64,1024]{1,0:T(8,128)(2,1)S(1)}, bf16[64,1024]{1,0:T(8,128)(2,1)S(1)}, u32[]{:S(2)}, u32[]{:S(2)}) collective-permute-start(bf16[64,1024]{1,0:T(8,128)(2,1)S(1)} %get-tuple-element.148.refs_1_), channel_id=1, source_target_pairs={{0,2},{2,0},{4,6},{6,4},{1,3},{3,1},{5,7},{7,5},{8,10},{10,8},{12,... | collective-permute-start | bytes 393224 | tf_op jit(solution)/shard_map/ppermute | solution.py:408
  50.0 12.4 %collective-permute-start.14 = (bf16[64,1024]{1,0:T(8,128)(2,1)S(1)}, bf16[64,1024]{1,0:T(8,128)(2,1)S(1)}, u32[]{:S(2)}, u32[]{:S(2)}) collective-permute-start(bf16[64,1024]{1,0:T(8,128)(2,1)S(1)} %get-tuple-element.148.refs_1_), channel_id=1, source_target_pairs={{0,4},{2,6},{4,0},{6,2},{1,5},{3,7},{5,1},{7,3},{8,12},{10,14},{12... | collective-permute-start | bytes 393224 | tf_op jit(solution)/shard_map/ppermute | solution.py:408
  51.0 11.4 %collective-permute-start.13 = (bf16[64,1024]{1,0:T(8,128)(2,1)S(1)}, bf16[64,1024]{1,0:T(8,128)(2,1)S(1)}, u32[]{:S(2)}, u32[]{:S(2)}) collective-permute-start(bf16[64,1024]{1,0:T(8,128)(2,1)S(1)} %get-tuple-element.147.refs_0_), channel_id=1, source_target_pairs={{0,2},{2,0},{4,6},{6,4},{1,3},{3,1},{5,7},{7,5},{8,10},{10,8},{12,... | collective-permute-start | bytes 393224 | tf_op jit(solution)/shard_map/ppermute | solution.py:408
  57.1 6.6 %collective-permute-start.10 = (bf16[64,1024]{1,0:T(8,128)(2,1)S(1)}, bf16[64,1024]{1,0:T(8,128)(2,1)S(1)}, u32[]{:S(2)}, u32[]{:S(2)}) collective-permute-start(bf16[64,1024]{1,0:T(8,128)(2,1)S(1)} %collective-permute-done.9.refs_4_), channel_id=1, source_target_pairs={{0,2},{2,0},{4,6},{6,4},{1,3},{3,1},{5,7},{7,5},{8,10},{10,8},{12,... | collective-permute-start | bytes 393224 | tf_op jit(solution)/shard_map/ppermute | solution.py:408
  66.2 9.3 %collective-permute-start.16 = (bf16[64,2048]{1,0:T(8,128)(2,1)S(1)}, bf16[64,2048]{1,0:T(8,128)(2,1)S(1)}, u32[]{:S(2)}, u32[]{:S(2)}) collective-permute-start(bf16[64,2048]{1,0:T(8,128)(2,1)S(1)} %shard_map.84.refs_0_), channel_id=1, source_target_pairs={{0,8},{8,16},{16,24},{1,9},{9,17},{17,25},{2,10},{10,18},{18,26},{... | collective-permute-start | bytes 786440 | tf_op jit(solution)/shard_map/ppermute | solution.py:605
  79.4 7.0 %collective-permute-start.19 = (bf16[72,1280]{1,0:T(8,128)(2,1)S(1)}, bf16[72,1280]{1,0:T(8,128)(2,1)S(1)}, u32[]{:S(2)}, u32[]{:S(2)}) collective-permute-start(bf16[72,1280]{1,0:T(8,128)(2,1)S(1)} %get-tuple-element.157), channel_id=1, source_target_pairs={{0,4},{2,6},{4,0},{6,2},{1,5},{3,7},{5,1},{7,3},{8,12},{10,14},{12... | collective-permute-start | bytes 552968 | tf_op jit(solution)/shard_map/ppermute | solution.py:408
  86.5 10.2 %collective-permute-start.21 = (bf16[72,1280]{1,0:T(8,128)(2,1)S(1)}, bf16[72,1280]{1,0:T(8,128)(2,1)S(1)}, u32[]{:S(2)}, u32[]{:S(2)}) collective-permute-start(bf16[72,1280]{1,0:T(8,128)(2,1)S(1)} %get-tuple-element.160), channel_id=1, source_target_pairs={{0,2},{2,0},{4,6},{6,4},{1,3},{3,1},{5,7},{7,5},{8,10},{10,8},{12,... | collective-permute-start | bytes 552968 | tf_op jit(solution)/shard_map/ppermute | solution.py:408
  87.0 8.7 %collective-permute-start.22 = (bf16[64,1280]{1,0:T(8,128)(2,1)S(1)}, bf16[64,1280]{1,0:T(8,128)(2,1)S(1)}, u32[]{:S(2)}, u32[]{:S(2)}) collective-permute-start(bf16[64,1280]{1,0:T(8,128)(2,1)S(1)} %get-tuple-element.161), channel_id=1, source_target_pairs={{0,2},{2,0},{4,6},{6,4},{1,3},{3,1},{5,7},{7,5},{8,10},{10,8},{12,... | collective-permute-start | bytes 491528 | tf_op jit(solution)/shard_map/ppermute | solution.py:408
  88.6 7.0 %collective-permute-start.18 = (bf16[64,1280]{1,0:T(8,128)(2,1)S(1)}, bf16[64,1280]{1,0:T(8,128)(2,1)S(1)}, u32[]{:S(2)}, u32[]{:S(2)}) collective-permute-start(bf16[64,1280]{1,0:T(8,128)(2,1)S(1)} %get-tuple-element.154), channel_id=1, source_target_pairs={{0,4},{2,6},{4,0},{6,2},{1,5},{3,7},{5,1},{7,3},{8,12},{10,14},{12... | collective-permute-start | bytes 491528 | tf_op jit(solution)/shard_map/ppermute | solution.py:408
  89.7 7.0 %collective-permute-start.23 = (bf16[64,1280]{1,0:T(8,128)(2,1)S(1)}, bf16[64,1280]{1,0:T(8,128)(2,1)S(1)}, u32[]{:S(2)}, u32[]{:S(2)}) collective-permute-start(bf16[64,1280]{1,0:T(8,128)(2,1)S(1)} %get-tuple-element.162), channel_id=1, source_target_pairs={{0,4},{2,6},{4,0},{6,2},{1,5},{3,7},{5,1},{7,3},{8,12},{10,14},{12... | collective-permute-start | bytes 491528 | tf_op jit(solution)/shard_map/ppermute | solution.py:408
  99.3 9.0 %collective-permute-start.28 = (bf16[64,1024]{1,0:T(8,128)(2,1)S(1)}, bf16[64,1024]{1,0:T(8,128)(2,1)S(1)}, u32[]{:S(2)}, u32[]{:S(2)}) collective-permute-start(bf16[64,1024]{1,0:T(8,128)(2,1)S(1)} %get-tuple-element.166.refs_0_), channel_id=1, source_target_pairs={{0,2},{2,0},{4,6},{6,4},{1,3},{3,1},{5,7},{7,5},{8,10},{10,8},{12,... | collective-permute-start | bytes 393224 | tf_op jit(solution)/shard_map/ppermute | solution.py:408
  101.0 7.3 %collective-permute-start.29 = (bf16[64,1024]{1,0:T(8,128)(2,1)S(1)}, bf16[64,1024]{1,0:T(8,128)(2,1)S(1)}, u32[]{:S(2)}, u32[]{:S(2)}) collective-permute-start(bf16[64,1024]{1,0:T(8,128)(2,1)S(1)} %get-tuple-element.167.refs_1_), channel_id=1, source_target_pairs={{0,4},{2,6},{4,0},{6,2},{1,5},{3,7},{5,1},{7,3},{8,12},{10,14},{12... | collective-permute-start | bytes 393224 | tf_op jit(solution)/shard_map/ppermute | solution.py:408
  112.2 10.2 %collective-permute-start.31 = (bf16[64,2048]{1,0:T(8,128)(2,1)S(1)}, bf16[64,2048]{1,0:T(8,128)(2,1)S(1)}, u32[]{:S(2)}, u32[]{:S(2)}) collective-permute-start(bf16[64,2048]{1,0:T(8,128)(2,1)S(1)} %shard_map.95.refs_1_), channel_id=1, source_target_pairs={{0,8},{8,16},{16,24},{1,9},{9,17},{17,25},{2,10},{10,18},{18,26},{... | collective-permute-start | bytes 786440 | tf_op jit(solution)/shard_map/ppermute | solution.py:605
  126.0 7.0 %collective-permute-start.34 = (bf16[72,1280]{1,0:T(8,128)(2,1)S(1)}, bf16[72,1280]{1,0:T(8,128)(2,1)S(1)}, u32[]{:S(2)}, u32[]{:S(2)}) collective-permute-start(bf16[72,1280]{1,0:T(8,128)(2,1)S(1)} %get-tuple-element.174), channel_id=1, source_target_pairs={{0,4},{2,6},{4,0},{6,2},{1,5},{3,7},{5,1},{7,3},{8,12},{10,14},{12... | collective-permute-start | bytes 552968 | tf_op jit(solution)/shard_map/ppermute | solution.py:408
  133.1 10.1 %collective-permute-start.36 = (bf16[72,1280]{1,0:T(8,128)(2,1)S(1)}, bf16[72,1280]{1,0:T(8,128)(2,1)S(1)}, u32[]{:S(2)}, u32[]{:S(2)}) collective-permute-start(bf16[72,1280]{1,0:T(8,128)(2,1)S(1)} %get-tuple-element.177), channel_id=1, source_target_pairs={{0,2},{2,0},{4,6},{6,4},{1,3},{3,1},{5,7},{7,5},{8,10},{10,8},{12,... | collective-permute-start | bytes 552968 | tf_op jit(solution)/shard_map/ppermute | solution.py:408
  134.0 8.2 %collective-permute-start.37 = (bf16[64,1280]{1,0:T(8,128)(2,1)S(1)}, bf16[64,1280]{1,0:T(8,128)(2,1)S(1)}, u32[]{:S(2)}, u32[]{:S(2)}) collective-permute-start(bf16[64,1280]{1,0:T(8,128)(2,1)S(1)} %get-tuple-element.178), channel_id=1, source_target_pairs={{0,2},{2,0},{4,6},{6,4},{1,3},{3,1},{5,7},{7,5},{8,10},{10,8},{12,... | collective-permute-start | bytes 491528 | tf_op jit(solution)/shard_map/ppermute | solution.py:408
  135.2 7.0 %collective-permute-start.33 = (bf16[64,1280]{1,0:T(8,128)(2,1)S(1)}, bf16[64,1280]{1,0:T(8,128)(2,1)S(1)}, u32[]{:S(2)}, u32[]{:S(2)}) collective-permute-start(bf16[64,1280]{1,0:T(8,128)(2,1)S(1)} %get-tuple-element.171), channel_id=1, source_target_pairs={{0,4},{2,6},{4,0},{6,2},{1,5},{3,7},{5,1},{7,3},{8,12},{10,14},{12... | collective-permute-start | bytes 491528 | tf_op jit(solution)/shard_map/ppermute | solution.py:408
  136.2 7.0 %collective-permute-start.38 = (bf16[64,1280]{1,0:T(8,128)(2,1)S(1)}, bf16[64,1280]{1,0:T(8,128)(2,1)S(1)}, u32[]{:S(2)}, u32[]{:S(2)}) collective-permute-start(bf16[64,1280]{1,0:T(8,128)(2,1)S(1)} %get-tuple-element.179), channel_id=1, source_target_pairs={{0,4},{2,6},{4,0},{6,2},{1,5},{3,7},{5,1},{7,3},{8,12},{10,14},{12... | collective-permute-start | bytes 491528 | tf_op jit(solution)/shard_map/ppermute | solution.py:408
  146.4 8.5 %collective-permute-start.43 = (bf16[64,1024]{1,0:T(8,128)(2,1)S(1)}, bf16[64,1024]{1,0:T(8,128)(2,1)S(1)}, u32[]{:S(2)}, u32[]{:S(2)}) collective-permute-start(bf16[64,1024]{1,0:T(8,128)(2,1)S(1)} %get-tuple-element.183.refs_0_), channel_id=1, source_target_pairs={{0,2},{2,0},{4,6},{6,4},{1,3},{3,1},{5,7},{7,5},{8,10},{10,8},{12,... | collective-permute-start | bytes 393224 | tf_op jit(solution)/shard_map/ppermute | solution.py:408
  147.5 7.3 %collective-permute-start.44 = (bf16[64,1024]{1,0:T(8,128)(2,1)S(1)}, bf16[64,1024]{1,0:T(8,128)(2,1)S(1)}, u32[]{:S(2)}, u32[]{:S(2)}) collective-permute-start(bf16[64,1024]{1,0:T(8,128)(2,1)S(1)} %get-tuple-element.184.refs_1_), channel_id=1, source_target_pairs={{0,4},{2,6},{4,0},{6,2},{1,5},{3,7},{5,1},{7,3},{8,12},{10,14},{12... | collective-permute-start | bytes 393224 | tf_op jit(solution)/shard_map/ppermute | solution.py:408
  150.1 6.0 %collective-permute-start.40 = (bf16[64,1024]{1,0:T(8,128)(2,1)S(1)}, bf16[64,1024]{1,0:T(8,128)(2,1)S(1)}, u32[]{:S(2)}, u32[]{:S(2)}) collective-permute-start(bf16[64,1024]{1,0:T(8,128)(2,1)S(1)} %collective-permute-done.39.refs_4_), channel_id=1, source_target_pairs={{0,2},{2,0},{4,6},{6,4},{1,3},{3,1},{5,7},{7,5},{8,10},{10,8},{12,... | collective-permute-start | bytes 393224 | tf_op jit(solution)/shard_map/ppermute | solution.py:408
  158.7 10.3 %collective-permute-start.46 = (bf16[64,2048]{1,0:T(8,128)(2,1)S(1)}, bf16[64,2048]{1,0:T(8,128)(2,1)S(1)}, u32[]{:S(2)}, u32[]{:S(2)}) collective-permute-start(bf16[64,2048]{1,0:T(8,128)(2,1)S(1)} %shard_map.105.refs_2_), channel_id=1, source_target_pairs={{0,8},{8,16},{16,24},{1,9},{9,17},{17,25},{2,10},{10,18},{18,26},{... | collective-permute-start | bytes 786440 | tf_op jit(solution)/shard_map/ppermute | solution.py:605
  172.5 7.0 %collective-permute-start.49 = (bf16[72,1280]{1,0:T(8,128)(2,1)S(1)}, bf16[72,1280]{1,0:T(8,128)(2,1)S(1)}, u32[]{:S(2)}, u32[]{:S(2)}) collective-permute-start(bf16[72,1280]{1,0:T(8,128)(2,1)S(1)} %get-tuple-element.191), channel_id=1, source_target_pairs={{0,4},{2,6},{4,0},{6,2},{1,5},{3,7},{5,1},{7,3},{8,12},{10,14},{12... | collective-permute-start | bytes 552968 | tf_op jit(solution)/shard_map/ppermute | solution.py:408
  179.6 10.2 %collective-permute-start.51 = (bf16[72,1280]{1,0:T(8,128)(2,1)S(1)}, bf16[72,1280]{1,0:T(8,128)(2,1)S(1)}, u32[]{:S(2)}, u32[]{:S(2)}) collective-permute-start(bf16[72,1280]{1,0:T(8,128)(2,1)S(1)} %get-tuple-element.194), channel_id=1, source_target_pairs={{0,2},{2,0},{4,6},{6,4},{1,3},{3,1},{5,7},{7,5},{8,10},{10,8},{12,... | collective-permute-start | bytes 552968 | tf_op jit(solution)/shard_map/ppermute | solution.py:408
  180.6 8.2 %collective-permute-start.52 = (bf16[64,1280]{1,0:T(8,128)(2,1)S(1)}, bf16[64,1280]{1,0:T(8,128)(2,1)S(1)}, u32[]{:S(2)}, u32[]{:S(2)}) collective-permute-start(bf16[64,1280]{1,0:T(8,128)(2,1)S(1)} %get-tuple-element.195), channel_id=1, source_target_pairs={{0,2},{2,0},{4,6},{6,4},{1,3},{3,1},{5,7},{7,5},{8,10},{10,8},{12,... | collective-permute-start | bytes 491528 | tf_op jit(solution)/shard_map/ppermute | solution.py:408
  181.7 7.1 %collective-permute-start.48 = (bf16[64,1280]{1,0:T(8,128)(2,1)S(1)}, bf16[64,1280]{1,0:T(8,128)(2,1)S(1)}, u32[]{:S(2)}, u32[]{:S(2)}) collective-permute-start(bf16[64,1280]{1,0:T(8,128)(2,1)S(1)} %get-tuple-element.188), channel_id=1, source_target_pairs={{0,4},{2,6},{4,0},{6,2},{1,5},{3,7},{5,1},{7,3},{8,12},{10,14},{12... | collective-permute-start | bytes 491528 | tf_op jit(solution)/shard_map/ppermute | solution.py:408
  182.8 7.0 %collective-permute-start.53 = (bf16[64,1280]{1,0:T(8,128)(2,1)S(1)}, bf16[64,1280]{1,0:T(8,128)(2,1)S(1)}, u32[]{:S(2)}, u32[]{:S(2)}) collective-permute-start(bf16[64,1280]{1,0:T(8,128)(2,1)S(1)} %get-tuple-element.196), channel_id=1, source_target_pairs={{0,4},{2,6},{4,0},{6,2},{1,5},{3,7},{5,1},{7,3},{8,12},{10,14},{12... | collective-permute-start | bytes 491528 | tf_op jit(solution)/shard_map/ppermute | solution.py:408
  192.9 8.5 %collective-permute-start.58 = (bf16[64,1024]{1,0:T(8,128)(2,1)S(1)}, bf16[64,1024]{1,0:T(8,128)(2,1)S(1)}, u32[]{:S(2)}, u32[]{:S(2)}) collective-permute-start(bf16[64,1024]{1,0:T(8,128)(2,1)S(1)} %get-tuple-element.200.refs_0_), channel_id=1, source_target_pairs={{0,2},{2,0},{4,6},{6,4},{1,3},{3,1},{5,7},{7,5},{8,10},{10,8},{12,... | collective-permute-start | bytes 393224 | tf_op jit(solution)/shard_map/ppermute | solution.py:408
  194.1 7.4 %collective-permute-start.59 = (bf16[64,1024]{1,0:T(8,128)(2,1)S(1)}, bf16[64,1024]{1,0:T(8,128)(2,1)S(1)}, u32[]{:S(2)}, u32[]{:S(2)}) collective-permute-start(bf16[64,1024]{1,0:T(8,128)(2,1)S(1)} %get-tuple-element.201.refs_1_), channel_id=1, source_target_pairs={{0,4},{2,6},{4,0},{6,2},{1,5},{3,7},{5,1},{7,3},{8,12},{10,14},{12... | collective-permute-start | bytes 393224 | tf_op jit(solution)/shard_map/ppermute | solution.py:408
  196.7 6.0 %collective-permute-start.55 = (bf16[64,1024]{1,0:T(8,128)(2,1)S(1)}, bf16[64,1024]{1,0:T(8,128)(2,1)S(1)}, u32[]{:S(2)}, u32[]{:S(2)}) collective-permute-start(bf16[64,1024]{1,0:T(8,128)(2,1)S(1)} %collective-permute-done.54.refs_4_), channel_id=1, source_target_pairs={{0,2},{2,0},{4,6},{6,4},{1,3},{3,1},{5,7},{7,5},{8,10},{10,8},{12,... | collective-permute-start | bytes 393224 | tf_op jit(solution)/shard_map/ppermute | solution.py:408
  205.3 10.2 %collective-permute-start.61 = (bf16[64,2048]{1,0:T(8,128)(2,1)S(1)}, bf16[64,2048]{1,0:T(8,128)(2,1)S(1)}, u32[]{:S(2)}, u32[]{:S(2)}) collective-permute-start(bf16[64,2048]{1,0:T(8,128)(2,1)S(1)} %shard_map.115.refs_3_), channel_id=1, source_target_pairs={{0,8},{8,16},{16,24},{1,9},{9,17},{17,25},{2,10},{10,18},{18,26},{... | collective-permute-start | bytes 786440 | tf_op jit(solution)/shard_map/ppermute | solution.py:605
  219.1 7.1 %collective-permute-start.64 = (bf16[72,1280]{1,0:T(8,128)(2,1)S(1)}, bf16[72,1280]{1,0:T(8,128)(2,1)S(1)}, u32[]{:S(2)}, u32[]{:S(2)}) collective-permute-start(bf16[72,1280]{1,0:T(8,128)(2,1)S(1)} %get-tuple-element.208), channel_id=1, source_target_pairs={{0,4},{2,6},{4,0},{6,2},{1,5},{3,7},{5,1},{7,3},{8,12},{10,14},{12... | collective-permute-start | bytes 552968 | tf_op jit(solution)/shard_map/ppermute | solution.py:408
  226.2 10.2 %collective-permute-start.66 = (bf16[72,1280]{1,0:T(8,128)(2,1)S(1)}, bf16[72,1280]{1,0:T(8,128)(2,1)S(1)}, u32[]{:S(2)}, u32[]{:S(2)}) collective-permute-start(bf16[72,1280]{1,0:T(8,128)(2,1)S(1)} %get-tuple-element.211), channel_id=1, source_target_pairs={{0,2},{2,0},{4,6},{6,4},{1,3},{3,1},{5,7},{7,5},{8,10},{10,8},{12,... | collective-permute-start | bytes 552968 | tf_op jit(solution)/shard_map/ppermute | solution.py:408
  227.1 8.2 %collective-permute-start.67 = (bf16[64,1280]{1,0:T(8,128)(2,1)S(1)}, bf16[64,1280]{1,0:T(8,128)(2,1)S(1)}, u32[]{:S(2)}, u32[]{:S(2)}) collective-permute-start(bf16[64,1280]{1,0:T(8,128)(2,1)S(1)} %get-tuple-element.212), channel_id=1, source_target_pairs={{0,2},{2,0},{4,6},{6,4},{1,3},{3,1},{5,7},{7,5},{8,10},{10,8},{12,... | collective-permute-start | bytes 491528 | tf_op jit(solution)/shard_map/ppermute | solution.py:408
  228.3 7.0 %collective-permute-start.63 = (bf16[64,1280]{1,0:T(8,128)(2,1)S(1)}, bf16[64,1280]{1,0:T(8,128)(2,1)S(1)}, u32[]{:S(2)}, u32[]{:S(2)}) collective-permute-start(bf16[64,1280]{1,0:T(8,128)(2,1)S(1)} %get-tuple-element.205), channel_id=1, source_target_pairs={{0,4},{2,6},{4,0},{6,2},{1,5},{3,7},{5,1},{7,3},{8,12},{10,14},{12... | collective-permute-start | bytes 491528 | tf_op jit(solution)/shard_map/ppermute | solution.py:408
  229.3 7.1 %collective-permute-start.68 = (bf16[64,1280]{1,0:T(8,128)(2,1)S(1)}, bf16[64,1280]{1,0:T(8,128)(2,1)S(1)}, u32[]{:S(2)}, u32[]{:S(2)}) collective-permute-start(bf16[64,1280]{1,0:T(8,128)(2,1)S(1)} %get-tuple-element.213), channel_id=1, source_target_pairs={{0,4},{2,6},{4,0},{6,2},{1,5},{3,7},{5,1},{7,3},{8,12},{10,14},{12... | collective-permute-start | bytes 491528 | tf_op jit(solution)/shard_map/ppermute | solution.py:408
  239.8 8.5 %collective-permute-start.73 = (bf16[64,1024]{1,0:T(8,128)(2,1)S(1)}, bf16[64,1024]{1,0:T(8,128)(2,1)S(1)}, u32[]{:S(2)}, u32[]{:S(2)}) collective-permute-start(bf16[64,1024]{1,0:T(8,128)(2,1)S(1)} %get-tuple-element.217.refs_0_), channel_id=1, source_target_pairs={{0,2},{2,0},{4,6},{6,4},{1,3},{3,1},{5,7},{7,5},{8,10},{10,8},{12,... | collective-permute-start | bytes 393224 | tf_op jit(solution)/shard_map/ppermute | solution.py:408
  241.0 7.3 %collective-permute-start.74 = (bf16[64,1024]{1,0:T(8,128)(2,1)S(1)}, bf16[64,1024]{1,0:T(8,128)(2,1)S(1)}, u32[]{:S(2)}, u32[]{:S(2)}) collective-permute-start(bf16[64,1024]{1,0:T(8,128)(2,1)S(1)} %get-tuple-element.218.refs_1_), channel_id=1, source_target_pairs={{0,4},{2,6},{4,0},{6,2},{1,5},{3,7},{5,1},{7,3},{8,12},{10,14},{12... | collective-permute-start | bytes 393224 | tf_op jit(solution)/shard_map/ppermute | solution.py:408
  243.6 6.0 %collective-permute-start.70 = (bf16[64,1024]{1,0:T(8,128)(2,1)S(1)}, bf16[64,1024]{1,0:T(8,128)(2,1)S(1)}, u32[]{:S(2)}, u32[]{:S(2)}) collective-permute-start(bf16[64,1024]{1,0:T(8,128)(2,1)S(1)} %collective-permute-done.69.refs_4_), channel_id=1, source_target_pairs={{0,2},{2,0},{4,6},{6,4},{1,3},{3,1},{5,7},{7,5},{8,10},{10,8},{12,... | collective-permute-start | bytes 393224 | tf_op jit(solution)/shard_map/ppermute | solution.py:408
  253.0 8.2 %collective-permute-start.77 = (bf16[64,2048]{1,0:T(8,128)(2,1)S(1)}, bf16[64,2048]{1,0:T(8,128)(2,1)S(1)}, u32[]{:S(2)}, u32[]{:S(2)}) collective-permute-start(bf16[64,2048]{1,0:T(8,128)(2,1)S(1)} %get-tuple-element.222), channel_id=1, source_target_pairs={{0,2},{1,0},{2,3},{3,1},{4,6},{5,4},{6,7},{7,5},{8,10},{9,8},{10,1... | collective-permute-start | bytes 786440 | tf_op jit(solution)/shard_map/ppermute | solution.py:438
  (34 other events, 152.3 us)

commit v2 on v1

--- a/solution.py
+++ b/solution.py
@@ -394,10 +394,12 @@
     offsets = [(dx, dy) for dx in range(size_gx) for dy in range(size_gy)][1:]
     offsets.sort(key=lambda o: (min(o[0], size_gx - o[0]) + min(o[1], size_gy - o[1])))
 
-    def chip_at(dx, dy):
-        x = index_gx + dx
-        y = index_gy + dy
-        return jnp.where(x >= size_gx, x - size_gx, x) * size_gy + jnp.where(y >= size_gy, y - size_gy, y)
+    def wrapped(index, step, size):
+        moved = index + step
+        return jnp.where(moved >= size, moved - size, moved)
+
+    def cut_at(value, index, size):
+        return lax.dynamic_slice_in_dim(value, index.astype(jnp.uint32), size, 0)
 
     def to_offset(value, dx, dy):
         pairs = [
@@ -408,6 +410,8 @@
         return lax.ppermute(value, ("gx", "gy"), pairs)
 
     def kv_start(chip):
+        if own_heads % group_size == 0:
+            return chip * used_cols
         return chip * own_heads // group_size * HD
 
     even = size_gy == size_gz == CHUNKS
@@ -417,14 +421,14 @@
             cut = block.reshape(size_gz, share, slab)
             pieces = []
             for j in range(CHUNKS):
-                spot = lax.rem(index_gy + j, size_gz)
+                spot = wrapped(index_gy, j, size_gz)
                 pairs = [
                     (a * size_gz + b, b * size_gz + (a + j) % size_gz) for a in range(size_gy) for b in range(size_gz)
                 ]
-                piece = lax.dynamic_index_in_dim(cut, spot, 0, keepdims=False)
+                piece = cut_at(cut, spot, 1)[0]
                 pieces.append(lax.ppermute(piece, ("gy", "gz"), pairs))
             return [
-                sum_of([(lax.rem(index_gz + size_gz - j, size_gz) == k, pieces[j]) for j in range(CHUNKS)])
+                sum_of([(index_gz == (k + j) % size_gz, pieces[j]) for j in range(CHUNKS)])
                 for k in range(CHUNKS)
             ]
 
@@ -460,12 +464,12 @@
             chosen = jnp.where(condition, value, chosen)
         return chosen
 
-    gain_slab = lax.dynamic_slice_in_dim(norm_gain[0], index_gy * slab, slab, 0)[None, :]
+    gain_slab = cut_at(norm_gain[0], index_gy * slab, slab)[None, :]
     own_bias = jnp.concatenate(
         [
-            lax.dynamic_slice_in_dim(q_bias[0], me * own_cols, own_cols, 0),
-            lax.dynamic_slice_in_dim(kv_bias[0, 0], kv_start(me), used_cols, 0),
-            lax.dynamic_slice_in_dim(kv_bias[0, 1], kv_start(me), used_cols, 0),
+            cut_at(q_bias[0], me * own_cols, own_cols),
+            cut_at(kv_bias[0, 0], kv_start(me), used_cols),
+            cut_at(kv_bias[0, 1], kv_start(me), used_cols),
         ]
     )[None, :]
 
@@ -491,17 +495,18 @@
     ]
     far_first = offsets[::-1]
     square = size_gx == size_gy == 2
-    targets = [chip_at(dx, dy) for dx, dy in far_first]
-    sources = [chip_at(size_gx - dx if dx else 0, size_gy - dy if dy else 0) for dx, dy in offsets]
+    steps_x = jnp.array([dx for dx, _ in far_first] + [-dx % size_gx for dx, _ in offsets] + [0], jnp.int32)
+    steps_y = jnp.array([dy for _, dy in far_first] + [-dy % size_gy for _, dy in offsets] + [0], jnp.int32)
+    chips = wrapped(index_gx, steps_x, size_gx) * size_gy + wrapped(index_gy, steps_y, size_gy)
     mine = 2 * len(offsets)
-    choice = [index_section, jnp.minimum(index_section, 1)]
-    picks = mine + 1 + len(choice)
+    choice = [jnp.stack([index_section, jnp.minimum(index_section, 1)])]
+    picks = mine + 3
     if even:
-        choice += [lax.rem(index_gz + j, size_gy) + index_section for j in range(CHUNKS)]
-        choice += [lax.rem(index_gy + size_gy - d, size_gz) for d in range(size_gz)]
-    table = jnp.stack(targets + sources + [me] + choice).astype(jnp.int32)
+        choice.append(wrapped(index_gz, jnp.arange(CHUNKS), size_gy) + index_section)
+        choice.append(wrapped(index_gy, -jnp.arange(size_gz) % size_gz, size_gz))
+    table = jnp.concatenate([chips, *choice]).astype(jnp.int32)
     early = [gain_slab, own_bias, *cosines, *sines, *masks]
-    (table, early, micro_inputs) = lax.optimization_barrier((table, early, micro_inputs))
+    (table, early) = lax.optimization_barrier((table, early))
     gain_slab, own_bias = early[:2]
     cosines, sines, masks = (early[2 + i * ticks : 2 + (i + 1) * ticks] for i in range(3))
     entering = [piece for m in range(micro_count) for piece in spread(micro_inputs[m])]

time: 264 us -> 259 us (0.981)
  waiting for transfers between devices: 87.4 us -> 81.2 us
    ppermute x2, waiting for transfers between devices: 6.18 us -> 0.01 us  [spread(): pieces.append(lax.ppermute(piece, ('gy', 'gz'), pairs))]
  transfers between devices with their start and end apart: 78 -> 78, of which waited for: 43 -> 42; matrix products, arithmetic and copies ran while one was open for 0% -> 2% of each run, Pallas kernels for 22% -> 22%
where the time goes in v2:
time: 259 us; the launch traced here: 258 us
  starting transfers between devices  86.2 us (33%)
  waiting for transfers between devices  81.2 us (31%)
  Pallas kernels  80.1 us (31%)
  local copies, waits for them, and re-layouts  4.28 us (2%)
  between operations  3.13 us (1%)
    ppermute x60, starting transfers between devices, to_offset(): return lax.ppermute(value, ('gx', 'gy'), pairs)  60.1 us
    ppermute x60, waiting for transfers between devices, to_offset(): return lax.ppermute(value, ('gx', 'gy'), pairs)  39.9 us
    pallas_call x15, Pallas kernels, project_block(): pl.pallas_call(kernel, out_shape=[jax.ShapeDtypeStruct((rows.shape[0] //...  25.3 us
    pallas_call x15, Pallas kernels, mix_blocks(): pl.pallas_call(kernel, out_shape=[jax.ShapeDtypeStruct((share, slab), jnp...  22.7 us
    ppermute x4, waiting for transfers between devices, body(): lax.ppermute(result, 'section', [(i, i + 1) for i in range(sections - 1)])  22.4 us
    ppermute x4, starting transfers between devices, body(): lax.ppermute(result, 'section', [(i, i + 1) for i in range(sections - 1)])  16.9 us
    ppermute x10, waiting for transfers between devices, around(): lax.ppermute(value, axis, [(i, (i + steps) % count) for i in range(count)])  13.7 us
    pallas_call x2, Pallas kernels, resident(): pl.pallas_call(kernel, out_shape=[(pltpu.SMEM if v.dtype == jnp.int32 els...  12.5 us
  transfers between devices with their start and end apart: 78, of which 42 were waited for; matrix products, arithmetic and copies ran while one was open for 2% of the time, Pallas kernels for 22%

profile of v2, /device:TPU:0, one launch (start us, length us, event | category | flops | bytes accessed | tf_op | source)
XLA Modules:
  0.0 257.5 jit_solution(14340867577382641930)
XLA Ops:
  9.8 3.9 %collective-permute-start.2 = (bf16[64,2048]{1,0:T(8,128)(2,1)S(1)}, bf16[64,2048]{1,0:T(8,128)(2,1)S(1)}, u32[]{:S(2)}, u32[]{:S(2)}) collective-permute-start(bf16[64,2048]{1,0:T(8,128)(2,1)S(1)} %get-tuple-element.227.refs_0_.x_ref), channel_id=1, source_target_pairs={{0,1},{1,0},{2,3},{3,2},{4,5},{5,4},{6,7},{7,6},{8,9},{9,8},{10,11... | collective-permute-start | bytes 786440 | tf_op jit(solution)/shard_map/ppermute | solution.py:359
  13.7 7.8 %shard_map.91 = (s32[13]{0:T(128)S(4)}, bf16[2048,5120]{1,0:T(8,128)(2,1)S(1)}) custom-call(s32[13]{0:T(128)S(1)} %concatenate.24.refs_0_, bf16[1,2048,4096]{2,1,0:T(8,128)(2,1)} %refs_1_.2, bf16[1,2,2048,512]{3,2,1,0:T(8,128)(2,1)} %refs_2_.1, f32[1,2048]{1,0:T(1,128)S(1)} %constant_dynamic-slice_fusion.3.refs_3_.gain_ref, ...), custom_call_target="tpu_custom_call" | custom-call | flops 4294967296 | tf_op jit(solution)/shard_map/pallas_call | solution.py:53
  21.5 2.1 shard_map.93
  23.6 2.0 collective-permute-start.4
  26.2 1.7 shard_map.96
  27.9 1.7 shard_map.95
  29.6 1.9 collective-permute-done.5.from_y_ref
  37.4 3.2 %collective-permute-done.7.refs_2_ = bf16[64,1280]{1,0:T(8,128)(2,1)S(1)} collective-permute-done((bf16[64,1280]{1,0:T(8,128)(2,1)S(1)}, bf16[64,1280]{1,0:T(8,128)(2,1)S(1)}, u32[]{:S(2)}, u32[]{:S(2)}) %collective-permute-start.7) | collective-permute-done | bytes 163872 | tf_op jit(solution)/shard_map/ppermute | solution.py:410
  41.6 2.3 shard_map.98
  48.0 4.7 %shard_map.92 = (s32[13]{0:T(128)S(4)}, bf16[1024,2048]{1,0:T(8,128)(2,1)S(1)}, bf16[1024,2048]{1,0:T(8,128)(2,1)S(1)}, bf16[1024,2048]{1,0:T(8,128)(2,1)S(1)}) custom-call(s32[13]{0:T(128)S(4)} %get-tuple-element.131.refs_0_.table_ref, bf16[1,4096,2048]{2,1,0:T(8,128)(2,1)} %w_ref.29), custom_call_target="tpu_custom_call" | custom-call | flops 4294967296 | tf_op jit(solution)/shard_map/pallas_call | solution.py:53
  55.3 2.5 shard_map.99.refs_6_
  61.7 3.5 %collective-permute-start.16 = (bf16[64,2048]{1,0:T(8,128)(2,1)S(1)}, bf16[64,2048]{1,0:T(8,128)(2,1)S(1)}, u32[]{:S(2)}, u32[]{:S(2)}) collective-permute-start(bf16[64,2048]{1,0:T(8,128)(2,1)S(1)} %shard_map.102.refs_0_), channel_id=1, source_target_pairs={{0,8},{8,16},{16,24},{1,9},{9,17},{17,25},{2,10},{10,18},{18,26},{... | collective-permute-start | bytes 786440 | tf_op jit(solution)/shard_map/ppermute | solution.py:610
  65.9 5.1 %collective-permute-done.16.refs_1_ = bf16[64,2048]{1,0:T(8,128)(2,1)S(1)} collective-permute-done((bf16[64,2048]{1,0:T(8,128)(2,1)S(1)}, bf16[64,2048]{1,0:T(8,128)(2,1)S(1)}, u32[]{:S(2)}, u32[]{:S(2)}) %collective-permute-start.16) | collective-permute-done | bytes 262176 | tf_op jit(solution)/shard_map/ppermute | solution.py:610
  72.9 2.1 shard_map.104
  76.5 1.7 shard_map.107
  78.2 1.7 shard_map.106
  79.9 2.1 collective-permute-done.20.from_y_ref
  86.2 1.7 shard_map.105.p_ref
  87.8 3.3 %collective-permute-done.22.refs_2_ = bf16[64,1280]{1,0:T(8,128)(2,1)S(1)} collective-permute-done((bf16[64,1280]{1,0:T(8,128)(2,1)S(1)}, bf16[64,1280]{1,0:T(8,128)(2,1)S(1)}, u32[]{:S(2)}, u32[]{:S(2)}) %collective-permute-start.22) | collective-permute-done | bytes 163872 | tf_op jit(solution)/shard_map/ppermute | solution.py:410
  101.3 2.5 shard_map.110.refs_6_
  107.6 4.4 %collective-permute-start.31 = (bf16[64,2048]{1,0:T(8,128)(2,1)S(1)}, bf16[64,2048]{1,0:T(8,128)(2,1)S(1)}, u32[]{:S(2)}, u32[]{:S(2)}) collective-permute-start(bf16[64,2048]{1,0:T(8,128)(2,1)S(1)} %shard_map.113.refs_1_), channel_id=1, source_target_pairs={{0,8},{8,16},{16,24},{1,9},{9,17},{17,25},{2,10},{10,18},{18,26},{... | collective-permute-start | bytes 786440 | tf_op jit(solution)/shard_map/ppermute | solution.py:610
  112.0 5.8 %collective-permute-done.31.refs_0_.x_ref = bf16[64,2048]{1,0:T(8,128)(2,1)S(1)} collective-permute-done((bf16[64,2048]{1,0:T(8,128)(2,1)S(1)}, bf16[64,2048]{1,0:T(8,128)(2,1)S(1)}, u32[]{:S(2)}, u32[]{:S(2)}) %collective-permute-start.31) | collective-permute-done | bytes 262176 | tf_op jit(solution)/shard_map/ppermute | solution.py:610
  119.4 2.1 shard_map.114
  123.4 1.7 shard_map.117
  125.1 1.7 shard_map.116
  126.8 1.7 collective-permute-done.35.from_y_ref
  132.7 1.7 shard_map.115.p_ref
  134.4 3.3 %collective-permute-done.37.refs_2_ = bf16[64,1280]{1,0:T(8,128)(2,1)S(1)} collective-permute-done((bf16[64,1280]{1,0:T(8,128)(2,1)S(1)}, bf16[64,1280]{1,0:T(8,128)(2,1)S(1)}, u32[]{:S(2)}, u32[]{:S(2)}) %collective-permute-start.37) | collective-permute-done | bytes 163872 | tf_op jit(solution)/shard_map/ppermute | solution.py:410
  147.8 2.5 shard_map.120.refs_6_
  154.2 4.6 %collective-permute-start.46 = (bf16[64,2048]{1,0:T(8,128)(2,1)S(1)}, bf16[64,2048]{1,0:T(8,128)(2,1)S(1)}, u32[]{:S(2)}, u32[]{:S(2)}) collective-permute-start(bf16[64,2048]{1,0:T(8,128)(2,1)S(1)} %shard_map.123.refs_2_), channel_id=1, source_target_pairs={{0,8},{8,16},{16,24},{1,9},{9,17},{17,25},{2,10},{10,18},{18,26},{... | collective-permute-start | bytes 786440 | tf_op jit(solution)/shard_map/ppermute | solution.py:610
  158.8 5.6 %collective-permute-done.46.refs_0_.x_ref = bf16[64,2048]{1,0:T(8,128)(2,1)S(1)} collective-permute-done((bf16[64,2048]{1,0:T(8,128)(2,1)S(1)}, bf16[64,2048]{1,0:T(8,128)(2,1)S(1)}, u32[]{:S(2)}, u32[]{:S(2)}) %collective-permute-start.46) | collective-permute-done | bytes 262176 | tf_op jit(solution)/shard_map/ppermute | solution.py:610
  165.9 2.1 shard_map.124
  169.9 1.7 shard_map.127
  171.6 1.7 shard_map.126
  173.3 1.7 collective-permute-done.50.from_y_ref
  179.2 1.7 shard_map.125.p_ref
  180.9 3.3 %collective-permute-done.52.refs_2_ = bf16[64,1280]{1,0:T(8,128)(2,1)S(1)} collective-permute-done((bf16[64,1280]{1,0:T(8,128)(2,1)S(1)}, bf16[64,1280]{1,0:T(8,128)(2,1)S(1)}, u32[]{:S(2)}, u32[]{:S(2)}) %collective-permute-start.52) | collective-permute-done | bytes 163872 | tf_op jit(solution)/shard_map/ppermute | solution.py:410
  194.3 2.5 shard_map.130.refs_6_
  200.7 4.4 %collective-permute-start.61 = (bf16[64,2048]{1,0:T(8,128)(2,1)S(1)}, bf16[64,2048]{1,0:T(8,128)(2,1)S(1)}, u32[]{:S(2)}, u32[]{:S(2)}) collective-permute-start(bf16[64,2048]{1,0:T(8,128)(2,1)S(1)} %shard_map.133.refs_3_), channel_id=1, source_target_pairs={{0,8},{8,16},{16,24},{1,9},{9,17},{17,25},{2,10},{10,18},{18,26},{... | collective-permute-start | bytes 786440 | tf_op jit(solution)/shard_map/ppermute | solution.py:610
  205.1 5.8 %collective-permute-done.61.refs_0_.x_ref = bf16[64,2048]{1,0:T(8,128)(2,1)S(1)} collective-permute-done((bf16[64,2048]{1,0:T(8,128)(2,1)S(1)}, bf16[64,2048]{1,0:T(8,128)(2,1)S(1)}, u32[]{:S(2)}, u32[]{:S(2)}) %collective-permute-start.61) | collective-permute-done | bytes 262176 | tf_op jit(solution)/shard_map/ppermute | solution.py:610
  212.5 2.1 shard_map.134
  216.5 1.7 shard_map.137
  218.2 1.7 shard_map.136
  225.8 1.7 shard_map.135.p_ref
  227.4 3.3 %collective-permute-done.67.refs_2_ = bf16[64,1280]{1,0:T(8,128)(2,1)S(1)} collective-permute-done((bf16[64,1280]{1,0:T(8,128)(2,1)S(1)}, bf16[64,1280]{1,0:T(8,128)(2,1)S(1)}, u32[]{:S(2)}, u32[]{:S(2)}) %collective-permute-start.67) | collective-permute-done | bytes 163872 | tf_op jit(solution)/shard_map/ppermute | solution.py:410
  241.3 2.5 shard_map.140.refs_6_
  248.4 3.0 %collective-permute-start.77 = (bf16[64,2048]{1,0:T(8,128)(2,1)S(1)}, bf16[64,2048]{1,0:T(8,128)(2,1)S(1)}, u32[]{:S(2)}, u32[]{:S(2)}) collective-permute-start(bf16[64,2048]{1,0:T(8,128)(2,1)S(1)} %get-tuple-element.220), channel_id=1, source_target_pairs={{0,2},{1,0},{2,3},{3,1},{4,6},{5,4},{6,7},{7,5},{8,10},{9,8},{10,1... | collective-permute-start | bytes 786440 | tf_op jit(solution)/shard_map/ppermute | solution.py:442
  251.5 5.2 %collective-permute-done.77.refs_1_ = bf16[64,2048]{1,0:T(8,128)(2,1)S(1)} collective-permute-done((bf16[64,2048]{1,0:T(8,128)(2,1)S(1)}, bf16[64,2048]{1,0:T(8,128)(2,1)S(1)}, u32[]{:S(2)}, u32[]{:S(2)}) %collective-permute-start.77) | collective-permute-done | bytes 262176 | tf_op jit(solution)/shard_map/ppermute | solution.py:442
  (194 shorter events, 115.7 us)
Async XLA Ops:
  1.1 8.7 %collective-permute-start = (bf16[64,2048]{1,0:T(8,128)(2,1)S(1)}, bf16[64,2048]{1,0:T(8,128)(2,1)S(1)}, u32[]{:S(2)}, u32[]{:S(2)}) collective-permute-start(bf16[64,2048]{1,0:T(8,128)(2,1)S(1)} %get-tuple-element.229), channel_id=1, source_target_pairs={{0,1},{1,3},{2,0},{3,2},{4,5},{5,7},{6,4},{7,6},{8,9},{9,11},{10,8... | collective-permute-start | bytes 786440 | tf_op jit(solution)/shard_map/ppermute | solution.py:429
  1.6 8.2 %collective-permute-start.1 = (bf16[64,2048]{1,0:T(8,128)(2,1)S(1)}, bf16[64,2048]{1,0:T(8,128)(2,1)S(1)}, u32[]{:S(2)}, u32[]{:S(2)}) collective-permute-start(bf16[64,2048]{1,0:T(8,128)(2,1)S(1)} %get-tuple-element.228), channel_id=1, source_target_pairs={{0,0},{1,2},{2,1},{3,3},{4,4},{5,6},{6,5},{7,7},{8,8},{9,10},{10,9... | collective-permute-start | bytes 786440 | tf_op jit(solution)/shard_map/ppermute | solution.py:429
  9.8 11.7 %collective-permute-start.2 = (bf16[64,2048]{1,0:T(8,128)(2,1)S(1)}, bf16[64,2048]{1,0:T(8,128)(2,1)S(1)}, u32[]{:S(2)}, u32[]{:S(2)}) collective-permute-start(bf16[64,2048]{1,0:T(8,128)(2,1)S(1)} %get-tuple-element.227.refs_0_.x_ref), channel_id=1, source_target_pairs={{0,1},{1,0},{2,3},{3,2},{4,5},{5,4},{6,7},{7,6},{8,9},{9,8},{10,11... | collective-permute-start | bytes 786440 | tf_op jit(solution)/shard_map/ppermute | solution.py:359
  23.6 7.9 %collective-permute-start.4 = (bf16[72,1280]{1,0:T(8,128)(2,1)S(1)}, bf16[72,1280]{1,0:T(8,128)(2,1)S(1)}, u32[]{:S(2)}, u32[]{:S(2)}) collective-permute-start(bf16[72,1280]{1,0:T(8,128)(2,1)S(1)} %get-tuple-element.138), channel_id=1, source_target_pairs={{0,4},{2,6},{4,0},{6,2},{1,5},{3,7},{5,1},{7,3},{8,12},{10,14},{12... | collective-permute-start | bytes 552968 | tf_op jit(solution)/shard_map/ppermute | solution.py:410
  31.6 10.0 %collective-permute-start.6 = (bf16[72,1280]{1,0:T(8,128)(2,1)S(1)}, bf16[72,1280]{1,0:T(8,128)(2,1)S(1)}, u32[]{:S(2)}, u32[]{:S(2)}) collective-permute-start(bf16[72,1280]{1,0:T(8,128)(2,1)S(1)} %get-tuple-element.141), channel_id=1, source_target_pairs={{0,2},{2,0},{4,6},{6,4},{1,3},{3,1},{5,7},{7,5},{8,10},{10,8},{12,... | collective-permute-start | bytes 552968 | tf_op jit(solution)/shard_map/ppermute | solution.py:410
  32.7 7.9 %collective-permute-start.7 = (bf16[64,1280]{1,0:T(8,128)(2,1)S(1)}, bf16[64,1280]{1,0:T(8,128)(2,1)S(1)}, u32[]{:S(2)}, u32[]{:S(2)}) collective-permute-start(bf16[64,1280]{1,0:T(8,128)(2,1)S(1)} %get-tuple-element.142), channel_id=1, source_target_pairs={{0,2},{2,0},{4,6},{6,4},{1,3},{3,1},{5,7},{7,5},{8,10},{10,8},{12,... | collective-permute-start | bytes 491528 | tf_op jit(solution)/shard_map/ppermute | solution.py:410
  33.7 6.9 %collective-permute-start.3 = (bf16[64,1280]{1,0:T(8,128)(2,1)S(1)}, bf16[64,1280]{1,0:T(8,128)(2,1)S(1)}, u32[]{:S(2)}, u32[]{:S(2)}) collective-permute-start(bf16[64,1280]{1,0:T(8,128)(2,1)S(1)} %get-tuple-element.135), channel_id=1, source_target_pairs={{0,4},{2,6},{4,0},{6,2},{1,5},{3,7},{5,1},{7,3},{8,12},{10,14},{12... | collective-permute-start | bytes 491528 | tf_op jit(solution)/shard_map/ppermute | solution.py:410
  34.4 7.2 %collective-permute-start.8 = (bf16[64,1280]{1,0:T(8,128)(2,1)S(1)}, bf16[64,1280]{1,0:T(8,128)(2,1)S(1)}, u32[]{:S(2)}, u32[]{:S(2)}) collective-permute-start(bf16[64,1280]{1,0:T(8,128)(2,1)S(1)} %get-tuple-element.143), channel_id=1, source_target_pairs={{0,4},{2,6},{4,0},{6,2},{1,5},{3,7},{5,1},{7,3},{8,12},{10,14},{12... | collective-permute-start | bytes 491528 | tf_op jit(solution)/shard_map/ppermute | solution.py:410
  43.9 10.4 %collective-permute-start.11 = (bf16[64,1024]{1,0:T(8,128)(2,1)S(1)}, bf16[64,1024]{1,0:T(8,128)(2,1)S(1)}, u32[]{:S(2)}, u32[]{:S(2)}) collective-permute-start(bf16[64,1024]{1,0:T(8,128)(2,1)S(1)} %get-tuple-element.146.refs_1_), channel_id=1, source_target_pairs={{0,2},{2,0},{4,6},{6,4},{1,3},{3,1},{5,7},{7,5},{8,10},{10,8},{12,... | collective-permute-start | bytes 393224 | tf_op jit(solution)/shard_map/ppermute | solution.py:410
  45.5 12.4 %collective-permute-start.14 = (bf16[64,1024]{1,0:T(8,128)(2,1)S(1)}, bf16[64,1024]{1,0:T(8,128)(2,1)S(1)}, u32[]{:S(2)}, u32[]{:S(2)}) collective-permute-start(bf16[64,1024]{1,0:T(8,128)(2,1)S(1)} %get-tuple-element.146.refs_1_), channel_id=1, source_target_pairs={{0,4},{2,6},{4,0},{6,2},{1,5},{3,7},{5,1},{7,3},{8,12},{10,14},{12... | collective-permute-start | bytes 393224 | tf_op jit(solution)/shard_map/ppermute | solution.py:410
  46.5 11.4 %collective-permute-start.13 = (bf16[64,1024]{1,0:T(8,128)(2,1)S(1)}, bf16[64,1024]{1,0:T(8,128)(2,1)S(1)}, u32[]{:S(2)}, u32[]{:S(2)}) collective-permute-start(bf16[64,1024]{1,0:T(8,128)(2,1)S(1)} %get-tuple-element.145.refs_0_), channel_id=1, source_target_pairs={{0,2},{2,0},{4,6},{6,4},{1,3},{3,1},{5,7},{7,5},{8,10},{10,8},{12,... | collective-permute-start | bytes 393224 | tf_op jit(solution)/shard_map/ppermute | solution.py:410
  52.8 6.4 %collective-permute-start.10 = (bf16[64,1024]{1,0:T(8,128)(2,1)S(1)}, bf16[64,1024]{1,0:T(8,128)(2,1)S(1)}, u32[]{:S(2)}, u32[]{:S(2)}) collective-permute-start(bf16[64,1024]{1,0:T(8,128)(2,1)S(1)} %collective-permute-done.9.refs_4_), channel_id=1, source_target_pairs={{0,2},{2,0},{4,6},{6,4},{1,3},{3,1},{5,7},{7,5},{8,10},{10,8},{12,... | collective-permute-start | bytes 393224 | tf_op jit(solution)/shard_map/ppermute | solution.py:410
  61.7 9.3 %collective-permute-start.16 = (bf16[64,2048]{1,0:T(8,128)(2,1)S(1)}, bf16[64,2048]{1,0:T(8,128)(2,1)S(1)}, u32[]{:S(2)}, u32[]{:S(2)}) collective-permute-start(bf16[64,2048]{1,0:T(8,128)(2,1)S(1)} %shard_map.102.refs_0_), channel_id=1, source_target_pairs={{0,8},{8,16},{16,24},{1,9},{9,17},{17,25},{2,10},{10,18},{18,26},{... | collective-permute-start | bytes 786440 | tf_op jit(solution)/shard_map/ppermute | solution.py:610
  74.9 7.0 %collective-permute-start.19 = (bf16[72,1280]{1,0:T(8,128)(2,1)S(1)}, bf16[72,1280]{1,0:T(8,128)(2,1)S(1)}, u32[]{:S(2)}, u32[]{:S(2)}) collective-permute-start(bf16[72,1280]{1,0:T(8,128)(2,1)S(1)} %get-tuple-element.155), channel_id=1, source_target_pairs={{0,4},{2,6},{4,0},{6,2},{1,5},{3,7},{5,1},{7,3},{8,12},{10,14},{12... | collective-permute-start | bytes 552968 | tf_op jit(solution)/shard_map/ppermute | solution.py:410
  82.0 10.2 %collective-permute-start.21 = (bf16[72,1280]{1,0:T(8,128)(2,1)S(1)}, bf16[72,1280]{1,0:T(8,128)(2,1)S(1)}, u32[]{:S(2)}, u32[]{:S(2)}) collective-permute-start(bf16[72,1280]{1,0:T(8,128)(2,1)S(1)} %get-tuple-element.158), channel_id=1, source_target_pairs={{0,2},{2,0},{4,6},{6,4},{1,3},{3,1},{5,7},{7,5},{8,10},{10,8},{12,... | collective-permute-start | bytes 552968 | tf_op jit(solution)/shard_map/ppermute | solution.py:410
  82.6 8.6 %collective-permute-start.22 = (bf16[64,1280]{1,0:T(8,128)(2,1)S(1)}, bf16[64,1280]{1,0:T(8,128)(2,1)S(1)}, u32[]{:S(2)}, u32[]{:S(2)}) collective-permute-start(bf16[64,1280]{1,0:T(8,128)(2,1)S(1)} %get-tuple-element.159), channel_id=1, source_target_pairs={{0,2},{2,0},{4,6},{6,4},{1,3},{3,1},{5,7},{7,5},{8,10},{10,8},{12,... | collective-permute-start | bytes 491528 | tf_op jit(solution)/shard_map/ppermute | solution.py:410
  84.1 7.1 %collective-permute-start.18 = (bf16[64,1280]{1,0:T(8,128)(2,1)S(1)}, bf16[64,1280]{1,0:T(8,128)(2,1)S(1)}, u32[]{:S(2)}, u32[]{:S(2)}) collective-permute-start(bf16[64,1280]{1,0:T(8,128)(2,1)S(1)} %get-tuple-element.152), channel_id=1, source_target_pairs={{0,4},{2,6},{4,0},{6,2},{1,5},{3,7},{5,1},{7,3},{8,12},{10,14},{12... | collective-permute-start | bytes 491528 | tf_op jit(solution)/shard_map/ppermute | solution.py:410
  85.2 7.0 %collective-permute-start.23 = (bf16[64,1280]{1,0:T(8,128)(2,1)S(1)}, bf16[64,1280]{1,0:T(8,128)(2,1)S(1)}, u32[]{:S(2)}, u32[]{:S(2)}) collective-permute-start(bf16[64,1280]{1,0:T(8,128)(2,1)S(1)} %get-tuple-element.160), channel_id=1, source_target_pairs={{0,4},{2,6},{4,0},{6,2},{1,5},{3,7},{5,1},{7,3},{8,12},{10,14},{12... | collective-permute-start | bytes 491528 | tf_op jit(solution)/shard_map/ppermute | solution.py:410
  95.0 8.9 %collective-permute-start.28 = (bf16[64,1024]{1,0:T(8,128)(2,1)S(1)}, bf16[64,1024]{1,0:T(8,128)(2,1)S(1)}, u32[]{:S(2)}, u32[]{:S(2)}) collective-permute-start(bf16[64,1024]{1,0:T(8,128)(2,1)S(1)} %get-tuple-element.164.refs_0_), channel_id=1, source_target_pairs={{0,2},{2,0},{4,6},{6,4},{1,3},{3,1},{5,7},{7,5},{8,10},{10,8},{12,... | collective-permute-start | bytes 393224 | tf_op jit(solution)/shard_map/ppermute | solution.py:410
  96.5 7.3 %collective-permute-start.29 = (bf16[64,1024]{1,0:T(8,128)(2,1)S(1)}, bf16[64,1024]{1,0:T(8,128)(2,1)S(1)}, u32[]{:S(2)}, u32[]{:S(2)}) collective-permute-start(bf16[64,1024]{1,0:T(8,128)(2,1)S(1)} %get-tuple-element.165.refs_1_), channel_id=1, source_target_pairs={{0,4},{2,6},{4,0},{6,2},{1,5},{3,7},{5,1},{7,3},{8,12},{10,14},{12... | collective-permute-start | bytes 393224 | tf_op jit(solution)/shard_map/ppermute | solution.py:410
  107.6 10.2 %collective-permute-start.31 = (bf16[64,2048]{1,0:T(8,128)(2,1)S(1)}, bf16[64,2048]{1,0:T(8,128)(2,1)S(1)}, u32[]{:S(2)}, u32[]{:S(2)}) collective-permute-start(bf16[64,2048]{1,0:T(8,128)(2,1)S(1)} %shard_map.113.refs_1_), channel_id=1, source_target_pairs={{0,8},{8,16},{16,24},{1,9},{9,17},{17,25},{2,10},{10,18},{18,26},{... | collective-permute-start | bytes 786440 | tf_op jit(solution)/shard_map/ppermute | solution.py:610
  121.5 7.0 %collective-permute-start.34 = (bf16[72,1280]{1,0:T(8,128)(2,1)S(1)}, bf16[72,1280]{1,0:T(8,128)(2,1)S(1)}, u32[]{:S(2)}, u32[]{:S(2)}) collective-permute-start(bf16[72,1280]{1,0:T(8,128)(2,1)S(1)} %get-tuple-element.172), channel_id=1, source_target_pairs={{0,4},{2,6},{4,0},{6,2},{1,5},{3,7},{5,1},{7,3},{8,12},{10,14},{12... | collective-permute-start | bytes 552968 | tf_op jit(solution)/shard_map/ppermute | solution.py:410
  128.6 10.2 %collective-permute-start.36 = (bf16[72,1280]{1,0:T(8,128)(2,1)S(1)}, bf16[72,1280]{1,0:T(8,128)(2,1)S(1)}, u32[]{:S(2)}, u32[]{:S(2)}) collective-permute-start(bf16[72,1280]{1,0:T(8,128)(2,1)S(1)} %get-tuple-element.175), channel_id=1, source_target_pairs={{0,2},{2,0},{4,6},{6,4},{1,3},{3,1},{5,7},{7,5},{8,10},{10,8},{12,... | collective-permute-start | bytes 552968 | tf_op jit(solution)/shard_map/ppermute | solution.py:410
  129.5 8.2 %collective-permute-start.37 = (bf16[64,1280]{1,0:T(8,128)(2,1)S(1)}, bf16[64,1280]{1,0:T(8,128)(2,1)S(1)}, u32[]{:S(2)}, u32[]{:S(2)}) collective-permute-start(bf16[64,1280]{1,0:T(8,128)(2,1)S(1)} %get-tuple-element.176), channel_id=1, source_target_pairs={{0,2},{2,0},{4,6},{6,4},{1,3},{3,1},{5,7},{7,5},{8,10},{10,8},{12,... | collective-permute-start | bytes 491528 | tf_op jit(solution)/shard_map/ppermute | solution.py:410
  130.7 7.0 %collective-permute-start.33 = (bf16[64,1280]{1,0:T(8,128)(2,1)S(1)}, bf16[64,1280]{1,0:T(8,128)(2,1)S(1)}, u32[]{:S(2)}, u32[]{:S(2)}) collective-permute-start(bf16[64,1280]{1,0:T(8,128)(2,1)S(1)} %get-tuple-element.169), channel_id=1, source_target_pairs={{0,4},{2,6},{4,0},{6,2},{1,5},{3,7},{5,1},{7,3},{8,12},{10,14},{12... | collective-permute-start | bytes 491528 | tf_op jit(solution)/shard_map/ppermute | solution.py:410
  131.7 7.0 %collective-permute-start.38 = (bf16[64,1280]{1,0:T(8,128)(2,1)S(1)}, bf16[64,1280]{1,0:T(8,128)(2,1)S(1)}, u32[]{:S(2)}, u32[]{:S(2)}) collective-permute-start(bf16[64,1280]{1,0:T(8,128)(2,1)S(1)} %get-tuple-element.177), channel_id=1, source_target_pairs={{0,4},{2,6},{4,0},{6,2},{1,5},{3,7},{5,1},{7,3},{8,12},{10,14},{12... | collective-permute-start | bytes 491528 | tf_op jit(solution)/shard_map/ppermute | solution.py:410
  141.9 8.5 %collective-permute-start.43 = (bf16[64,1024]{1,0:T(8,128)(2,1)S(1)}, bf16[64,1024]{1,0:T(8,128)(2,1)S(1)}, u32[]{:S(2)}, u32[]{:S(2)}) collective-permute-start(bf16[64,1024]{1,0:T(8,128)(2,1)S(1)} %get-tuple-element.181.refs_0_), channel_id=1, source_target_pairs={{0,2},{2,0},{4,6},{6,4},{1,3},{3,1},{5,7},{7,5},{8,10},{10,8},{12,... | collective-permute-start | bytes 393224 | tf_op jit(solution)/shard_map/ppermute | solution.py:410
  143.0 7.3 %collective-permute-start.44 = (bf16[64,1024]{1,0:T(8,128)(2,1)S(1)}, bf16[64,1024]{1,0:T(8,128)(2,1)S(1)}, u32[]{:S(2)}, u32[]{:S(2)}) collective-permute-start(bf16[64,1024]{1,0:T(8,128)(2,1)S(1)} %get-tuple-element.182.refs_1_), channel_id=1, source_target_pairs={{0,4},{2,6},{4,0},{6,2},{1,5},{3,7},{5,1},{7,3},{8,12},{10,14},{12... | collective-permute-start | bytes 393224 | tf_op jit(solution)/shard_map/ppermute | solution.py:410
  145.6 6.0 %collective-permute-start.40 = (bf16[64,1024]{1,0:T(8,128)(2,1)S(1)}, bf16[64,1024]{1,0:T(8,128)(2,1)S(1)}, u32[]{:S(2)}, u32[]{:S(2)}) collective-permute-start(bf16[64,1024]{1,0:T(8,128)(2,1)S(1)} %collective-permute-done.39.refs_4_), channel_id=1, source_target_pairs={{0,2},{2,0},{4,6},{6,4},{1,3},{3,1},{5,7},{7,5},{8,10},{10,8},{12,... | collective-permute-start | bytes 393224 | tf_op jit(solution)/shard_map/ppermute | solution.py:410
  154.2 10.2 %collective-permute-start.46 = (bf16[64,2048]{1,0:T(8,128)(2,1)S(1)}, bf16[64,2048]{1,0:T(8,128)(2,1)S(1)}, u32[]{:S(2)}, u32[]{:S(2)}) collective-permute-start(bf16[64,2048]{1,0:T(8,128)(2,1)S(1)} %shard_map.123.refs_2_), channel_id=1, source_target_pairs={{0,8},{8,16},{16,24},{1,9},{9,17},{17,25},{2,10},{10,18},{18,26},{... | collective-permute-start | bytes 786440 | tf_op jit(solution)/shard_map/ppermute | solution.py:610
  168.0 7.0 %collective-permute-start.49 = (bf16[72,1280]{1,0:T(8,128)(2,1)S(1)}, bf16[72,1280]{1,0:T(8,128)(2,1)S(1)}, u32[]{:S(2)}, u32[]{:S(2)}) collective-permute-start(bf16[72,1280]{1,0:T(8,128)(2,1)S(1)} %get-tuple-element.189), channel_id=1, source_target_pairs={{0,4},{2,6},{4,0},{6,2},{1,5},{3,7},{5,1},{7,3},{8,12},{10,14},{12... | collective-permute-start | bytes 552968 | tf_op jit(solution)/shard_map/ppermute | solution.py:410
  175.1 10.1 %collective-permute-start.51 = (bf16[72,1280]{1,0:T(8,128)(2,1)S(1)}, bf16[72,1280]{1,0:T(8,128)(2,1)S(1)}, u32[]{:S(2)}, u32[]{:S(2)}) collective-permute-start(bf16[72,1280]{1,0:T(8,128)(2,1)S(1)} %get-tuple-element.192), channel_id=1, source_target_pairs={{0,2},{2,0},{4,6},{6,4},{1,3},{3,1},{5,7},{7,5},{8,10},{10,8},{12,... | collective-permute-start | bytes 552968 | tf_op jit(solution)/shard_map/ppermute | solution.py:410
  176.1 8.2 %collective-permute-start.52 = (bf16[64,1280]{1,0:T(8,128)(2,1)S(1)}, bf16[64,1280]{1,0:T(8,128)(2,1)S(1)}, u32[]{:S(2)}, u32[]{:S(2)}) collective-permute-start(bf16[64,1280]{1,0:T(8,128)(2,1)S(1)} %get-tuple-element.193), channel_id=1, source_target_pairs={{0,2},{2,0},{4,6},{6,4},{1,3},{3,1},{5,7},{7,5},{8,10},{10,8},{12,... | collective-permute-start | bytes 491528 | tf_op jit(solution)/shard_map/ppermute | solution.py:410
  177.2 7.0 %collective-permute-start.48 = (bf16[64,1280]{1,0:T(8,128)(2,1)S(1)}, bf16[64,1280]{1,0:T(8,128)(2,1)S(1)}, u32[]{:S(2)}, u32[]{:S(2)}) collective-permute-start(bf16[64,1280]{1,0:T(8,128)(2,1)S(1)} %get-tuple-element.186), channel_id=1, source_target_pairs={{0,4},{2,6},{4,0},{6,2},{1,5},{3,7},{5,1},{7,3},{8,12},{10,14},{12... | collective-permute-start | bytes 491528 | tf_op jit(solution)/shard_map/ppermute | solution.py:410
  178.2 7.0 %collective-permute-start.53 = (bf16[64,1280]{1,0:T(8,128)(2,1)S(1)}, bf16[64,1280]{1,0:T(8,128)(2,1)S(1)}, u32[]{:S(2)}, u32[]{:S(2)}) collective-permute-start(bf16[64,1280]{1,0:T(8,128)(2,1)S(1)} %get-tuple-element.194), channel_id=1, source_target_pairs={{0,4},{2,6},{4,0},{6,2},{1,5},{3,7},{5,1},{7,3},{8,12},{10,14},{12... | collective-permute-start | bytes 491528 | tf_op jit(solution)/shard_map/ppermute | solution.py:410
  188.4 8.4 %collective-permute-start.58 = (bf16[64,1024]{1,0:T(8,128)(2,1)S(1)}, bf16[64,1024]{1,0:T(8,128)(2,1)S(1)}, u32[]{:S(2)}, u32[]{:S(2)}) collective-permute-start(bf16[64,1024]{1,0:T(8,128)(2,1)S(1)} %get-tuple-element.198.refs_0_), channel_id=1, source_target_pairs={{0,2},{2,0},{4,6},{6,4},{1,3},{3,1},{5,7},{7,5},{8,10},{10,8},{12,... | collective-permute-start | bytes 393224 | tf_op jit(solution)/shard_map/ppermute | solution.py:410
  189.5 7.3 %collective-permute-start.59 = (bf16[64,1024]{1,0:T(8,128)(2,1)S(1)}, bf16[64,1024]{1,0:T(8,128)(2,1)S(1)}, u32[]{:S(2)}, u32[]{:S(2)}) collective-permute-start(bf16[64,1024]{1,0:T(8,128)(2,1)S(1)} %get-tuple-element.199.refs_1_), channel_id=1, source_target_pairs={{0,4},{2,6},{4,0},{6,2},{1,5},{3,7},{5,1},{7,3},{8,12},{10,14},{12... | collective-permute-start | bytes 393224 | tf_op jit(solution)/shard_map/ppermute | solution.py:410
  192.1 6.0 %collective-permute-start.55 = (bf16[64,1024]{1,0:T(8,128)(2,1)S(1)}, bf16[64,1024]{1,0:T(8,128)(2,1)S(1)}, u32[]{:S(2)}, u32[]{:S(2)}) collective-permute-start(bf16[64,1024]{1,0:T(8,128)(2,1)S(1)} %collective-permute-done.54.refs_4_), channel_id=1, source_target_pairs={{0,2},{2,0},{4,6},{6,4},{1,3},{3,1},{5,7},{7,5},{8,10},{10,8},{12,... | collective-permute-start | bytes 393224 | tf_op jit(solution)/shard_map/ppermute | solution.py:410
  200.7 10.3 %collective-permute-start.61 = (bf16[64,2048]{1,0:T(8,128)(2,1)S(1)}, bf16[64,2048]{1,0:T(8,128)(2,1)S(1)}, u32[]{:S(2)}, u32[]{:S(2)}) collective-permute-start(bf16[64,2048]{1,0:T(8,128)(2,1)S(1)} %shard_map.133.refs_3_), channel_id=1, source_target_pairs={{0,8},{8,16},{16,24},{1,9},{9,17},{17,25},{2,10},{10,18},{18,26},{... | collective-permute-start | bytes 786440 | tf_op jit(solution)/shard_map/ppermute | solution.py:610
  214.5 7.0 %collective-permute-start.64 = (bf16[72,1280]{1,0:T(8,128)(2,1)S(1)}, bf16[72,1280]{1,0:T(8,128)(2,1)S(1)}, u32[]{:S(2)}, u32[]{:S(2)}) collective-permute-start(bf16[72,1280]{1,0:T(8,128)(2,1)S(1)} %get-tuple-element.206), channel_id=1, source_target_pairs={{0,4},{2,6},{4,0},{6,2},{1,5},{3,7},{5,1},{7,3},{8,12},{10,14},{12... | collective-permute-start | bytes 552968 | tf_op jit(solution)/shard_map/ppermute | solution.py:410
  221.6 10.2 %collective-permute-start.66 = (bf16[72,1280]{1,0:T(8,128)(2,1)S(1)}, bf16[72,1280]{1,0:T(8,128)(2,1)S(1)}, u32[]{:S(2)}, u32[]{:S(2)}) collective-permute-start(bf16[72,1280]{1,0:T(8,128)(2,1)S(1)} %get-tuple-element.209), channel_id=1, source_target_pairs={{0,2},{2,0},{4,6},{6,4},{1,3},{3,1},{5,7},{7,5},{8,10},{10,8},{12,... | collective-permute-start | bytes 552968 | tf_op jit(solution)/shard_map/ppermute | solution.py:410
  222.6 8.2 %collective-permute-start.67 = (bf16[64,1280]{1,0:T(8,128)(2,1)S(1)}, bf16[64,1280]{1,0:T(8,128)(2,1)S(1)}, u32[]{:S(2)}, u32[]{:S(2)}) collective-permute-start(bf16[64,1280]{1,0:T(8,128)(2,1)S(1)} %get-tuple-element.210), channel_id=1, source_target_pairs={{0,2},{2,0},{4,6},{6,4},{1,3},{3,1},{5,7},{7,5},{8,10},{10,8},{12,... | collective-permute-start | bytes 491528 | tf_op jit(solution)/shard_map/ppermute | solution.py:410
  223.7 7.1 %collective-permute-start.63 = (bf16[64,1280]{1,0:T(8,128)(2,1)S(1)}, bf16[64,1280]{1,0:T(8,128)(2,1)S(1)}, u32[]{:S(2)}, u32[]{:S(2)}) collective-permute-start(bf16[64,1280]{1,0:T(8,128)(2,1)S(1)} %get-tuple-element.203), channel_id=1, source_target_pairs={{0,4},{2,6},{4,0},{6,2},{1,5},{3,7},{5,1},{7,3},{8,12},{10,14},{12... | collective-permute-start | bytes 491528 | tf_op jit(solution)/shard_map/ppermute | solution.py:410
  224.8 7.0 %collective-permute-start.68 = (bf16[64,1280]{1,0:T(8,128)(2,1)S(1)}, bf16[64,1280]{1,0:T(8,128)(2,1)S(1)}, u32[]{:S(2)}, u32[]{:S(2)}) collective-permute-start(bf16[64,1280]{1,0:T(8,128)(2,1)S(1)} %get-tuple-element.211), channel_id=1, source_target_pairs={{0,4},{2,6},{4,0},{6,2},{1,5},{3,7},{5,1},{7,3},{8,12},{10,14},{12... | collective-permute-start | bytes 491528 | tf_op jit(solution)/shard_map/ppermute | solution.py:410
  235.3 8.5 %collective-permute-start.73 = (bf16[64,1024]{1,0:T(8,128)(2,1)S(1)}, bf16[64,1024]{1,0:T(8,128)(2,1)S(1)}, u32[]{:S(2)}, u32[]{:S(2)}) collective-permute-start(bf16[64,1024]{1,0:T(8,128)(2,1)S(1)} %get-tuple-element.215.refs_0_), channel_id=1, source_target_pairs={{0,2},{2,0},{4,6},{6,4},{1,3},{3,1},{5,7},{7,5},{8,10},{10,8},{12,... | collective-permute-start | bytes 393224 | tf_op jit(solution)/shard_map/ppermute | solution.py:410
  236.5 7.4 %collective-permute-start.74 = (bf16[64,1024]{1,0:T(8,128)(2,1)S(1)}, bf16[64,1024]{1,0:T(8,128)(2,1)S(1)}, u32[]{:S(2)}, u32[]{:S(2)}) collective-permute-start(bf16[64,1024]{1,0:T(8,128)(2,1)S(1)} %get-tuple-element.216.refs_1_), channel_id=1, source_target_pairs={{0,4},{2,6},{4,0},{6,2},{1,5},{3,7},{5,1},{7,3},{8,12},{10,14},{12... | collective-permute-start | bytes 393224 | tf_op jit(solution)/shard_map/ppermute | solution.py:410
  239.1 6.0 %collective-permute-start.70 = (bf16[64,1024]{1,0:T(8,128)(2,1)S(1)}, bf16[64,1024]{1,0:T(8,128)(2,1)S(1)}, u32[]{:S(2)}, u32[]{:S(2)}) collective-permute-start(bf16[64,1024]{1,0:T(8,128)(2,1)S(1)} %collective-permute-done.69.refs_4_), channel_id=1, source_target_pairs={{0,2},{2,0},{4,6},{6,4},{1,3},{3,1},{5,7},{7,5},{8,10},{10,8},{12,... | collective-permute-start | bytes 393224 | tf_op jit(solution)/shard_map/ppermute | solution.py:410
  248.4 8.2 %collective-permute-start.77 = (bf16[64,2048]{1,0:T(8,128)(2,1)S(1)}, bf16[64,2048]{1,0:T(8,128)(2,1)S(1)}, u32[]{:S(2)}, u32[]{:S(2)}) collective-permute-start(bf16[64,2048]{1,0:T(8,128)(2,1)S(1)} %get-tuple-element.220), channel_id=1, source_target_pairs={{0,2},{1,0},{2,3},{3,1},{4,6},{5,4},{6,7},{7,5},{8,10},{9,8},{10,1... | collective-permute-start | bytes 786440 | tf_op jit(solution)/shard_map/ppermute | solution.py:442
  (34 other events, 155.3 us)
